TPU v7x, 32 devices: a whole 2x2x4 slice. The times are simulated.
32 devices in a mesh: patch: 16 (over z, x, core), tp: 2 (over y).
Axes of the slice: x: 2, y: 2, z: 4, core: 2. Of those that a mesh axis runs over, the one named last changes fastest.
Arguments:
- resid_corrupt: bfloat16 [512, 4096], P(None, 'tp'), may hold values from -6 to 6
- resid_clean: bfloat16 [2, 512, 4096], P(None, 'patch', 'tp'), may hold values from -6 to 6
- patch_level: int32 [16], P('patch'), may hold values from 0 to 1
- patch_mask: int32 [16, 128], P('patch'), may hold values 0 or 1
- norm_gain: bfloat16 [4096], P('tp'), may hold values from 0.099609375 to 1.8984375
- final_gain: bfloat16 [4096], P('tp'), may hold values from 0.099609375 to 1.8984375
- w_query: bfloat16 [4096, 4096], P('patch', 'tp'), may hold values from -1 to 1
- w_key: bfloat16 [4096, 1024], P('patch', 'tp'), may hold values from -1 to 1
- w_value: bfloat16 [4096, 1024], P('patch', 'tp'), may hold values from -0.09375 to 0.09375
- w_out: bfloat16 [4096, 4096], P('tp', 'patch'), may hold values from -0.09375 to 0.09375
- unembed: bfloat16 [128256, 4096], P(('patch', 'tp')), may hold values from -0.09375 to 0.09375
- scored_ids: int32 [256], replicated, may hold values from 0 to 128255
- base_logits: float32 [512, 256], P('tp'), may hold values from -6 to 6
Outputs:
- logit_shift: float32 [16, 512, 256], P('patch', 'tp')
All inputs are finite; a program needn't handle non-finite values. No bound on the sum of `patch_mask` on one device may be relied on, other than what follows from the above.
Results may differ from a plain program's by a relative error of at most 0.01.
The roundings to bfloat16 on the way count: a program that leaves them out, or rounds other values in their place, can miss the bound.
Values may be sent and summed in bfloat16 or wider, within the bound.
No kernel may reach another device: no remote copies, remote signals or barrier semaphores. Data moves between devices by JAX's collectives and lax.ppermute only.
A program may use at most 192 MiB of HBM per device.

v0:
```python
import jax
import jax.numpy as jnp
from jax import lax
from jax.experimental import pallas as pl
from jax.experimental.pallas import tpu as pltpu
from jax.sharding import PartitionSpec as P


D = 4096
HD = 128
SEQ = 128
PROMPTS = 4
HALF = HD // 2

EPSILON = 1e-05
THETA = 500000.0


def is_power(n):
    return n & (n - 1) == 0


def xor_pairs(n, flip):
    return [(i, i ^ flip) for i in range(n)]


def swap_tp(x):
    return lax.ppermute(x, "tp", [(0, 1), (1, 0)])


def over_tp(x):
    n = lax.axis_size("tp")
    if n == 2:
        first = lax.axis_index("tp") == 0
        other = swap_tp(x)
        return [jnp.where(first, x, other), jnp.where(first, other, x)]
    every = lax.all_gather(x, "tp", axis=0)
    return [every[i] for i in range(n)]


def exchange_tp(x):
    n = lax.axis_size("tp")
    if n == 2:
        me = lax.axis_index("tp")
        first = me == 0
        mine = lax.dynamic_index_in_dim(x, me, 0, keepdims=False)
        other = swap_tp(lax.dynamic_index_in_dim(x, 1 - me, 0, keepdims=False))
        return [jnp.where(first, mine, other), jnp.where(first, other, mine)]
    got = lax.all_to_all(x, "tp", 0, 0, tiled=False)
    return [got[i] for i in range(n)]


def reduce_patch(x):
    n = lax.axis_size("patch")
    me = lax.axis_index("patch")
    flip = 1
    while flip < n:
        pairs = x.reshape((x.shape[0] // 2, 2) + x.shape[1:])
        bit = (me // flip) % 2
        send = lax.dynamic_index_in_dim(pairs, 1 - bit, 1, keepdims=False)
        keep = lax.dynamic_index_in_dim(pairs, bit, 1, keepdims=False)
        x = keep + lax.ppermute(send, "patch", xor_pairs(n, flip))
        flip *= 2
    return x[0]


def rope_angles(first, count):
    index = (first + lax.iota(jnp.int32, count)).astype(jnp.float32)
    freqs = THETA ** (-(index * 2.0 / HD))
    return lax.iota(jnp.int32, SEQ).astype(jnp.float32)[:, None] * freqs[None, :]


def rotate(values, first):
    count = values.shape[1] // 2
    angles = rope_angles(first, count)
    cosine = jnp.tile(jnp.cos(angles), (values.shape[0] // SEQ, 1))
    sine = jnp.tile(jnp.sin(angles), (values.shape[0] // SEQ, 1))
    lower, upper = values[:, :count], values[:, count:]
    return jnp.concatenate([lower * cosine - upper * sine, upper * cosine + lower * sine], axis=1)


def attend_body(q_ref, k_ref, v_ref, m_ref, o_ref):
    heads = q_ref.shape[0]
    patched = m_ref[0] > 0.5

    def pick(ref, *lead):
        clean = ref[lead + (1, 0)].astype(jnp.float32)
        corrupt = ref[lead + (0, 0)].astype(jnp.float32)
        return jnp.where(patched, clean, corrupt).astype(jnp.bfloat16)

    keys = pick(k_ref)
    values = pick(v_ref)
    queries = jnp.concatenate([pick(q_ref, h) for h in range(heads)], axis=0)
    scores = lax.dot_general(
        queries, keys, (((1,), (1,)), ((), ())), preferred_element_type=jnp.float32
    ) * HD ** (-0.5)
    row = lax.broadcasted_iota(jnp.int32, scores.shape, 0) % SEQ
    col = lax.broadcasted_iota(jnp.int32, scores.shape, 1)
    scores = jnp.where(row >= col, scores, -1e30)
    top = jnp.max(scores, axis=1, keepdims=True)
    weights = jnp.exp(scores - top)
    probs = (weights / jnp.sum(weights, axis=1, keepdims=True)).astype(jnp.bfloat16)
    out = jnp.dot(probs, values, preferred_element_type=jnp.float32).astype(jnp.bfloat16)
    for h in range(heads):
        o_ref[0, :, h * HD : (h + 1) * HD] = out[h * SEQ : (h + 1) * SEQ]


def attend(q, k, v, masks):
    heads, _, prompts = q.shape[:3]
    groups = masks.shape[0]
    return pl.pallas_call(
        attend_body,
        grid=(prompts, groups),
        in_specs=[
            pl.BlockSpec((heads, 2, 1, SEQ, HD), lambda p, g: (0, 0, p, 0, 0)),
            pl.BlockSpec((2, 1, SEQ, HD), lambda p, g: (0, p, 0, 0)),
            pl.BlockSpec((2, 1, SEQ, HD), lambda p, g: (0, p, 0, 0)),
            pl.BlockSpec((1, SEQ, HD), lambda p, g: (g, 0, 0)),
        ],
        out_specs=pl.BlockSpec((1, SEQ, heads * HD), lambda p, g: (g, p, 0)),
        out_shape=jax.ShapeDtypeStruct((groups, prompts * SEQ, heads * HD), jnp.bfloat16),
        name="attend",
    )(q, k, v, masks)


def splice_body(place_ref, corrupt_a, corrupt_b, clean_a, clean_b, late_ref, code_ref, o_ref):
    code = code_ref[...]
    code = jnp.concatenate([code, code], axis=1)
    corrupt = jnp.concatenate([corrupt_a[...], corrupt_b[...]], axis=1).astype(jnp.float32)
    clean = jnp.concatenate([clean_a[...], clean_b[...]], axis=1).astype(jnp.float32)
    rows = jnp.where(code == 1, clean, corrupt)
    rows = jnp.where(code == 2, late_ref[...].astype(jnp.float32), rows)
    o_ref[...] = rows.astype(jnp.bfloat16)


def splice(place, corrupt, clean, code, columns):
    tokens, sub = code.shape

    def lane(q, place):
        return 2 * q + place[0]

    return pl.pallas_call(
        splice_body,
        grid_spec=pltpu.PrefetchScalarGridSpec(
            num_scalar_prefetch=1,
            grid=(columns // (2 * sub),),
            in_specs=[
                pl.BlockSpec((tokens, sub), lambda i, s: (0, lane(2 * i, s))),
                pl.BlockSpec((tokens, sub), lambda i, s: (0, lane(2 * i + 1, s))),
                pl.BlockSpec((tokens, sub), lambda i, s: (0, lane(2 * i, s))),
                pl.BlockSpec((tokens, sub), lambda i, s: (0, lane(2 * i + 1, s))),
                pl.BlockSpec((tokens, 2 * sub), lambda i, s: (0, D // (2 * sub) + i)),
                pl.BlockSpec((tokens, sub), lambda i, s: (0, 0)),
            ],
            out_specs=pl.BlockSpec((tokens, 2 * sub), lambda i, s: (0, i)),
        ),
        out_shape=jax.ShapeDtypeStruct((tokens, columns), jnp.bfloat16),
        name="splice",
    )(place, corrupt, corrupt, clean, clean, clean, code)


def finish_body(place_ref, *refs):
    heads = [refs[:4], refs[4:8]]
    w_ref, base_ref, code_ref, gain_ref, score_ref = refs[8:13]
    o_ref, sum_ref = refs[13:]
    step = pl.program_id(0)
    rows = heads[0][0].shape[1]
    code = code_ref[...]
    code = jnp.concatenate([code, code], axis=1)
    base = base_ref[...].astype(jnp.float32)
    residual = base
    for half in range(2):
        term = None
        for slot in range(4):
            at = pl.multiple_of((half * 4 + (place_ref[1] ^ slot)) * rows, rows)
            part = jnp.dot(
                heads[half][slot][...], w_ref[pl.ds(at, rows), :], preferred_element_type=jnp.float32
            )
            term = part if term is None else term + part
        residual = residual + term.astype(jnp.bfloat16).astype(jnp.float32)
    residual = jnp.where(code == 2, base, residual)
    final = (residual * gain_ref[...].astype(jnp.float32)).astype(jnp.bfloat16)
    score = jnp.concatenate([score_ref[0], score_ref[1]], axis=1)
    logits = lax.dot_general(
        final, score, (((1,), (1,)), ((), ())), preferred_element_type=jnp.float32
    )
    squares = residual * residual
    squares = squares[:, : squares.shape[1] // 2] + squares[:, squares.shape[1] // 2 :]

    @pl.when(step == 0)
    def _():
        o_ref[...] = logits
        sum_ref[...] = squares

    @pl.when(step > 0)
    def _():
        o_ref[...] += logits
        sum_ref[...] += squares

    @pl.when(step == pl.num_programs(0) - 1)
    def _():
        total = jnp.sum(sum_ref[...], axis=1, keepdims=True)
        sum_ref[...] = jnp.broadcast_to(total, sum_ref.shape)


def finish(place, heads, weights, base, code, gain, score):
    tokens, block = heads[0].shape
    columns = weights.shape[1]
    scored, sub = score.shape[1:]

    whole = pl.BlockSpec((tokens, block), lambda i, s: (0, 0))
    return pl.pallas_call(
        finish_body,
        grid_spec=pltpu.PrefetchScalarGridSpec(
            num_scalar_prefetch=1,
            grid=(columns // (2 * sub),),
            in_specs=[whole] * 8
            + [
                pl.BlockSpec((weights.shape[0], 2 * sub), lambda i, s: (0, i)),
                pl.BlockSpec((tokens, 2 * sub), lambda i, s: (0, i)),
                pl.BlockSpec((tokens, sub), lambda i, s: (0, 0)),
                pl.BlockSpec((1, 2 * sub), lambda i, s: (0, i)),
                pl.BlockSpec((2, scored, sub), lambda i, s: (i, 0, 0)),
            ],
            out_specs=[
                pl.BlockSpec((tokens, scored), lambda i, s: (0, 0)),
                pl.BlockSpec((tokens, sub), lambda i, s: (0, 0)),
            ],
        ),
        out_shape=[
            jax.ShapeDtypeStruct((tokens, scored), jnp.float32),
            jax.ShapeDtypeStruct((tokens, sub), jnp.float32),
        ],
        name="finish",
    )(place, *heads, weights, base, code, gain, score)


def on_device(
    resid_corrupt,
    resid_clean,
    patch_level,
    patch_mask,
    norm_gain,
    final_gain,
    w_query,
    w_key,
    w_value,
    w_out,
    unembed,
    scored_ids,
    base_logits,
):
    n_p, n_t = lax.axis_size("patch"), lax.axis_size("tp")
    me_p, me_t = lax.axis_index("patch"), lax.axis_index("tp")
    tokens = resid_corrupt.shape[0]
    slices_t = n_p // n_t
    sub = D // (n_p * n_t)
    kv_here = w_key.shape[1] // HD
    spread = n_p // kv_here
    per_kv = w_query.shape[1] // w_key.shape[1]
    me_a, me_b = me_p // kv_here, me_p % kv_here
    bf16, f32 = jnp.bfloat16, jnp.float32
    fused = n_t == 2 and kv_here == 4 and sub == HD

    depth = w_query.shape[0]
    cut = spread // per_kv
    q_cols = w_query.reshape(depth, kv_here, per_kv, 2, cut, HALF // cut)
    q_cols = q_cols.transpose(2, 4, 1, 0, 3, 5).reshape(n_p, depth, HD // cut)
    k_cols = w_key.reshape(depth, kv_here, 2, spread, HALF // spread)
    k_cols = k_cols.transpose(3, 1, 0, 2, 4).reshape(n_p, depth, HD // spread)
    v_cols = w_value.reshape(depth, kv_here, spread, HD // spread)
    v_cols = v_cols.transpose(2, 1, 0, 3).reshape(n_p, depth, HD // spread)
    send = jnp.concatenate([q_cols, k_cols, v_cols], axis=2)
    width_q, width_kv = HD // cut, HD // spread
    weights = lax.all_to_all(send, "patch", 0, 0, tiled=True).reshape(D, send.shape[2])

    corrupt_full = jnp.concatenate(over_tp(resid_corrupt), axis=1)
    rows_here = resid_clean.shape[1]
    clean_rows = jnp.concatenate(over_tp(resid_clean[0]), axis=1)
    late_parts = exchange_tp(
        resid_clean[1].reshape(rows_here, slices_t, n_t, sub).transpose(2, 0, 1, 3)
    )
    late_rows_here = jnp.concatenate(late_parts, axis=1).reshape(rows_here, n_p * sub)
    both_sites = lax.all_gather(
        jnp.concatenate([clean_rows, late_rows_here], axis=1), "patch", axis=0, tiled=True
    )
    clean_full = both_sites[:, :D]
    gain_full = jnp.concatenate(over_tp(norm_gain)).astype(f32)
    final_full = jnp.concatenate(over_tp(final_gain)).astype(f32)

    out_block = w_out.reshape(w_out.shape[0], n_t, sub).transpose(1, 0, 2)
    if fused:
        swapped = swap_tp(lax.dynamic_index_in_dim(out_block, 1 - me_t, 0, keepdims=False))
        out_rows = jnp.concatenate(
            [lax.dynamic_index_in_dim(out_block, me_t, 0, keepdims=False), swapped], axis=0
        )
    else:
        out_rows = jnp.concatenate(exchange_tp(out_block), axis=0)
    out_cols = lax.all_gather(out_rows, "patch", axis=1, tiled=True)

    def project(rows):
        rows = rows.astype(f32)
        scale = lax.rsqrt(jnp.mean(rows * rows, axis=1, keepdims=True) + EPSILON)
        normed = (rows * scale * gain_full).astype(bf16)
        return jnp.dot(normed, weights, preferred_element_type=f32)

    projected = jnp.concatenate([project(corrupt_full), project(clean_full)], axis=0)
    piece = jnp.concatenate(
        [
            rotate(projected[:, :width_q], (me_a % cut) * (HALF // cut)),
            rotate(projected[:, width_q : width_q + width_kv], me_a * (HALF // spread)),
            projected[:, width_q + width_kv :],
        ],
        axis=1,
    ).astype(bf16)

    if is_power(spread) and spread <= 8:
        got = [piece] + [
            lax.ppermute(piece, "patch", xor_pairs(n_p, k * kv_here)) for k in range(1, spread)
        ]
        got = jnp.stack(got)
        pieces = jnp.stack(
            [lax.dynamic_index_in_dim(got, me_a ^ i, 0, keepdims=False) for i in range(spread)]
        )
    else:
        sets = [[a * kv_here + b for a in range(spread)] for b in range(kv_here)]
        pieces = lax.all_gather(piece, "patch", axis=0, axis_index_groups=sets)
    all_rows = piece.shape[0]
    q = pieces[:, :, :width_q].reshape(per_kv, cut, all_rows, 2, HALF // cut)
    q = q.transpose(0, 2, 3, 1, 4).reshape(per_kv, 2, PROMPTS, SEQ, HD)
    k = pieces[:, :, width_q : width_q + width_kv].reshape(spread, all_rows, 2, HALF // spread)
    k = k.transpose(1, 2, 0, 3).reshape(2, PROMPTS, SEQ, HD)
    v = pieces[:, :, width_q + width_kv :].transpose(1, 0, 2).reshape(2, PROMPTS, SEQ, HD)

    early_here = (patch_mask * (patch_level[0] == 0)).astype(f32)
    early = [early_here] + [
        lax.ppermute(early_here, "patch", xor_pairs(n_p, j)) for j in range(1, kv_here)
    ]
    early = jnp.concatenate(early, axis=0)
    masks = jnp.broadcast_to(early[:, :, None], (kv_here, SEQ, HD))
    attended = attend(q, k, v, masks)

    mine = [attended[0]] + [
        lax.ppermute(attended[j], "patch", xor_pairs(n_p, j)) for j in range(1, kv_here)
    ]

    rows_dev = unembed.shape[0]
    local = scored_ids - lax.axis_index(("patch", "tp")) * rows_dev
    owned = (local >= 0) & (local < rows_dev)
    picked = jnp.where(
        owned[:, None], jnp.take(unembed, jnp.clip(local, 0, rows_dev - 1), axis=0), 0
    ).astype(bf16)
    scored = picked.shape[0]
    block = reduce_patch(picked.reshape(scored, n_p, n_t * sub).transpose(1, 0, 2))
    by_sub = block.reshape(scored, n_t, sub).transpose(1, 0, 2)
    if fused:
        score = lax.dynamic_index_in_dim(by_sub, me_t, 0, keepdims=False) + swap_tp(
            lax.dynamic_index_in_dim(by_sub, 1 - me_t, 0, keepdims=False)
        )
    else:
        score = sum(exchange_tp(by_sub))
    score = lax.all_gather(score, "patch", axis=0, tiled=True).reshape(n_p, scored, sub)

    row_mask = jnp.tile(patch_mask[0], PROMPTS) == 1
    share = tokens // n_t
    final_own = lax.dynamic_index_in_dim(
        final_full.reshape(n_p, n_t, sub), me_t, 1, keepdims=False
    ).reshape(1, n_p * sub)
    if fused:
        heads = mine + [swap_tp(x) for x in mine]
        code = jnp.where(row_mask, 1 + patch_level[0], 0)
        code = jnp.broadcast_to(code[:, None], (tokens, sub))
        place = jnp.stack([me_t, me_b]).astype(jnp.int32)
        base = splice(place, corrupt_full, both_sites, code, n_p * sub)
        parts = finish(place, heads, out_cols, base, code, final_own, score)
        logits, squares = (x.reshape(n_t, share, -1) for x in parts)

        def halves(x):
            return (
                lax.dynamic_index_in_dim(x, me_t, 0, keepdims=False),
                lax.dynamic_index_in_dim(x, 1 - me_t, 0, keepdims=False),
            )

        logits_keep, logits_send = halves(logits)
        squares_keep, squares_send = halves(squares[:, :, 0])
        square_sum = squares_keep + swap_tp(squares_send)
        total = logits_keep + swap_tp(logits_send.astype(bf16)).astype(f32)
        scaling = lax.rsqrt(square_sum / D + EPSILON)[:, None]
        return (total * scaling - base_logits)[None]

    def in_order(slots):
        stacked = jnp.stack(slots)
        return jnp.concatenate(
            [
                lax.dynamic_index_in_dim(stacked, me_b ^ j, 0, keepdims=False)
                for j in range(kv_here)
            ],
            axis=1,
        )

    by_slot = [over_tp(x) for x in mine]
    rows_t = w_out.shape[0]
    early_rows = jnp.tile(early_here[0], PROMPTS)[:, None] > 0.5
    late_rows = (row_mask & (patch_level[0] == 1))[:, None]

    def own_features(x):
        own = lax.dynamic_index_in_dim(x.reshape(tokens, n_p, n_t, sub), me_t, 2, keepdims=False)
        return own.reshape(tokens, n_p * sub)

    residual = jnp.where(early_rows, own_features(clean_full), own_features(corrupt_full))
    residual = residual.astype(f32)
    for i in range(n_t):
        term = jnp.dot(
            in_order([slot[i] for slot in by_slot]),
            out_cols[i * rows_t : (i + 1) * rows_t],
            preferred_element_type=f32,
        )
        residual = residual + term.astype(bf16).astype(f32)
    residual = jnp.where(late_rows, both_sites[:, D:].astype(f32), residual)
    squares = jnp.sum(residual * residual, axis=1)
    final_block = (residual * final_own).astype(bf16).reshape(tokens, n_p, sub)
    logits = jnp.einsum("rpj,psj->rs", final_block, score, preferred_element_type=f32)
    total = sum(exchange_tp(logits.reshape(n_t, share, -1)))
    square_sum = sum(exchange_tp(squares.reshape(n_t, share)))
    scaling = lax.rsqrt(square_sum / D + EPSILON)[:, None]
    return (total * scaling - base_logits)[None]


def solution(mesh):
    placed = (
        P(None, "tp"),
        P(None, "patch", "tp"),
        P("patch"),
        P("patch", None),
        P("tp"),
        P("tp"),
        P("patch", "tp"),
        P("patch", "tp"),
        P("patch", "tp"),
        P("tp", "patch"),
        P(("patch", "tp"), None),
        P(),
        P("tp", None),
    )
    return jax.shard_map(
        on_device, mesh=mesh, in_specs=placed, out_specs=P("patch", "tp", None), check_vma=False
    )
```

profile of v0, /device:TPU:20, one launch (start us, length us, event | category | flops | bytes accessed | tf_op | source)
XLA Modules:
  0.0 373.8 jit_solution(18295889671663647811)
XLA Ops:
  8.5 1.5 collective-permute-start.2
  10.0 2.9 collective-permute-done.3
  13.1 1.6 collective-permute-done.2
  15.6 13.3 %gather_fusion = bf16[256,4096]{1,0:T(8,128)(2,1)S(1)} fusion(bf16[4008,4096]{1,0:T(8,128)(2,1)} %param.23, s32[1024]{0:T(1024)S(1)} %pad_clamp_fusion), kind=kCustom, calls=%fused_computation | custom fusion | bytes 4195328 | tf_op jit(solution)/shard_map/jit(_take)/gather | solution.py:351
  29.4 1.3 copy-done.3
  30.9 2.6 collective-permute-done.19
  33.5 1.3 bitcast_add_fusion
  34.9 1.7 collective-permute-start.20
  36.6 14.2 %collective-permute-done.20 = bf16[4,256,256]{2,1,0:T(8,128)(2,1)S(1)} collective-permute-done((bf16[4,256,256]{2,1,0:T(8,128)(2,1)S(1)}, bf16[4,256,256]{2,1,0:T(8,128)(2,1)S(1)}, u32[]{:S(2)}, u32[]{:S(2)}) %collective-permute-start.20) | collective-permute-done | bytes 524320 | tf_op jit(solution)/shard_map/ppermute | solution.py:62
  50.9 1.9 collective-permute-start.21
  52.8 17.1 %collective-permute-done.21 = bf16[2,256,256]{2,1,0:T(8,128)(2,1)S(1)} collective-permute-done((bf16[2,256,256]{2,1,0:T(8,128)(2,1)S(1)}, bf16[2,256,256]{2,1,0:T(8,128)(2,1)S(1)}, u32[]{:S(2)}, u32[]{:S(2)}) %collective-permute-start.21) | collective-permute-done | bytes 262176 | tf_op jit(solution)/shard_map/ppermute | solution.py:62
  70.0 2.1 collective-permute-start.22
  72.1 9.6 %collective-permute-done.22 = bf16[1,256,256]{2,1,0:T(8,128)(2,1)S(1)} collective-permute-done((bf16[1,256,256]{2,1,0:T(8,128)(2,1)S(1)}, bf16[1,256,256]{2,1,0:T(8,128)(2,1)S(1)}, u32[]{:S(2)}, u32[]{:S(2)}) %collective-permute-start.22) | collective-permute-done | bytes 131104 | tf_op jit(solution)/shard_map/ppermute | solution.py:62
  83.2 3.2 collective-permute-done.23
  87.4 2.2 constant_dynamic-slice_fusion.6
  90.8 11.4 %collective-permute-done.17 = bf16[2048,128]{1,0:T(8,128)(2,1)S(1)} collective-permute-done((bf16[2048,128]{1,0:T(8,128)(2,1)S(1)}, bf16[2048,128]{1,0:T(8,128)(2,1)S(1)}, u32[]{:S(2)}, u32[]{:S(2)}) %collective-permute-start.17) | collective-permute-done | bytes 524320 | tf_op jit(solution)/shard_map/ppermute | solution.py:28
  106.0 1.3 pad_maximum_fusion.1
  107.3 7.8 %all-to-all-start = ((bf16[16,256,192]{1,2,0:T(8,128)(2,1)}), bf16[16,256,192]{1,2,0:T(8,128)(2,1)}, u32[]{:S(2)}, u32[]{:S(2)}) async-start(bf16[16,256,192]{1,2,0:T(8,128)(2,1)} %pad_maximum_fusion.1), calls=%async_computation | async-start | bytes 3145728 | tf_op jit(solution)/shard_map/all_to_all | solution.py:275
  117.5 31.7 %collective-permute-done.1 = bf16[2048]{0:T(1024)(128)(2,1)S(1)} collective-permute-done((bf16[2048]{0:T(1024)(128)(2,1)S(1)}, bf16[2048]{0:T(1024)(128)(2,1)S(1)}, u32[]{:S(2)}, u32[]{:S(2)}) %collective-permute-start.1) | collective-permute-done | bytes 4128 | tf_op jit(solution)/shard_map/ppermute | solution.py:28
  149.3 2.5 broadcast_select_fusion.1
  153.2 19.8 %all-to-all-done = bf16[16,256,192]{1,2,0:T(8,128)(2,1)} async-done(((bf16[16,256,192]{1,2,0:T(8,128)(2,1)}), bf16[16,256,192]{1,2,0:T(8,128)(2,1)}, u32[]{:S(2)}, u32[]{:S(2)}) %all-to-all-start) | async-done | bytes 1572896 | tf_op jit(solution)/shard_map/all_to_all | solution.py:275
  173.0 1.7 copy.71
  175.9 1.7 fusion.8
  177.7 3.2 fusion.3
  180.9 3.8 %fusion.6 = f32[512,192]{0,1:T(8,128)S(1)} fusion(bf16[4096,192]{0,1:T(8,128)(2,1)S(1)} %bitcast.208, f32[512]{0:T(512)S(1)} %add_rsqrt_fusion, f32[4096]{0:T(1024)S(1)} %maximum_convert_fusion, bf16[512,6144]{1,0:T(8,128)(2,1)} %all-gather.4.cloned.1.call-done.clean_a.clean_b.late_ref), kind=kOutput, calls=%fused_computation.11 | convolution fusion | flops 813694976 | bytes 6178816 | tf_op jit(solution)/shard_map/dot_general | solution.py:305
  188.4 3.4 collective-permute-start.6
  194.4 1.8 collective-permute-done.8
  196.7 14.1 %collective-permute-done.4 = bf16[1024,192]{0,1:T(8,128)(2,1)S(1)} collective-permute-done((bf16[1024,192]{0,1:T(8,128)(2,1)}, bf16[1024,192]{0,1:T(8,128)(2,1)S(1)}, u32[]{:S(2)}, u32[]{:S(2)}) %collective-permute-start.4) | collective-permute-done | bytes 393248 | tf_op jit(solution)/shard_map/ppermute | solution.py:319
  210.8 13.2 %collective-permute-done.5 = bf16[1024,192]{0,1:T(8,128)(2,1)S(1)} collective-permute-done((bf16[1024,192]{0,1:T(8,128)(2,1)}, bf16[1024,192]{0,1:T(8,128)(2,1)S(1)}, u32[]{:S(2)}, u32[]{:S(2)}) %collective-permute-start.5) | collective-permute-done | bytes 393248 | tf_op jit(solution)/shard_map/ppermute | solution.py:319
  224.0 37.2 %collective-permute-done.6 = bf16[1024,192]{0,1:T(8,128)(2,1)} collective-permute-done((bf16[1024,192]{0,1:T(8,128)(2,1)}, bf16[1024,192]{0,1:T(8,128)(2,1)}, u32[]{:S(2)}, u32[]{:S(2)}) %collective-permute-start.6) | collective-permute-done | bytes 393248 | tf_op jit(solution)/shard_map/ppermute | solution.py:319
  265.0 1.8 copy.46.k_ref
  270.2 1.3 copy.44
  272.3 13.3 %attend.1 = bf16[4,512,512]{2,1,0:T(8,128)(2,1)} custom-call(bf16[4,2,4,128,128]{4,3,2,1,0:T(8,128)(2,1)} %bitcast.199, bf16[2,4,128,128]{3,2,1,0:T(8,128)(2,1)} %copy.46.k_ref, bf16[2,4,128,128]{3,2,1,0:T(8,128)(2,1)} %copy.47.v_ref, f32[4,128,128]{2,1,0:T(8,128)} %broadcast_in_dim.57.m_ref), custom_call_target="tpu_custom_call" | custom-call | tf_op jit(solution)/shard_map/attend/pallas_call | solution.py:111
  285.6 1.8 slice_bitcast_fusion
  287.6 1.8 collective-permute-start.12
  290.6 1.9 collective-permute-start.13
  292.6 9.9 %collective-permute-done.11.refs_2_ = bf16[512,512]{1,0:T(8,128)(2,1)} collective-permute-done((bf16[512,512]{1,0:T(8,128)(2,1)S(1)}, bf16[512,512]{1,0:T(8,128)(2,1)}, u32[]{:S(2)}, u32[]{:S(2)}) %collective-permute-start.11) | collective-permute-done | bytes 524320 | tf_op jit(solution)/shard_map/ppermute | solution.py:344
  302.5 1.9 collective-permute-start.15
  304.4 8.2 %collective-permute-done.12.refs_3_ = bf16[512,512]{1,0:T(8,128)(2,1)} collective-permute-done((bf16[512,512]{1,0:T(8,128)(2,1)S(1)}, bf16[512,512]{1,0:T(8,128)(2,1)}, u32[]{:S(2)}, u32[]{:S(2)}) %collective-permute-start.12) | collective-permute-done | bytes 524320 | tf_op jit(solution)/shard_map/ppermute | solution.py:344
  312.6 1.9 collective-permute-start.16
  314.6 2.5 pad_maximum_fusion.corrupt_a.corrupt_b
  317.9 7.8 %splice.1.refs_9_ = bf16[512,2048]{1,0:T(8,128)(2,1)} custom-call(s32[2]{0:T(128)} %pad_add_fusion.place_ref, bf16[512,4096]{1,0:T(8,128)(2,1)} %pad_maximum_fusion.corrupt_a.corrupt_b, bf16[512,4096]{1,0:T(8,128)(2,1)} %pad_maximum_fusion.corrupt_a.corrupt_b, bf16[512,6144]{1,0:T(8,128)(2,1)} %all-gather.4.cloned.1.call-done.clean_a.clean_b.late_ref, ...), custom_call_target="tpu_custom_call" | custom-call | tf_op jit(solution)/shard_map/splice/pallas_call | solution.py:142
  325.8 2.2 collective-permute-done.15.refs_6_
  327.9 10.8 %collective-permute-done.16.refs_7_ = bf16[512,512]{1,0:T(8,128)(2,1)} collective-permute-done((bf16[512,512]{1,0:T(8,128)(2,1)}, bf16[512,512]{1,0:T(8,128)(2,1)}, u32[]{:S(2)}, u32[]{:S(2)}) %collective-permute-start.16) | collective-permute-done | bytes 524320 | tf_op jit(solution)/shard_map/ppermute | solution.py:28
  338.8 17.9 %finish.1 = (f32[512,256]{1,0:T(8,128)}, f32[512,128]{1,0:T(8,128)}) custom-call(s32[2]{0:T(128)} %pad_add_fusion.place_ref, bf16[512,512]{1,0:T(8,128)(2,1)} %copy-done.5, bf16[512,512]{1,0:T(8,128)(2,1)} %copy-done.11, bf16[512,512]{1,0:T(8,128)(2,1)} %collective-permute-done.11.refs_2_, bf16[512,512]{1,0:T(8,128)(2,1)} %collective-permute-done.12.refs_3_, ...), custom_call_target="tpu_custom_call" | custom-call | tf_op jit(solution)/shard_map/finish/pallas_call | solution.py:212
  357.7 1.8 collective-permute-start.25
  361.3 4.2 %collective-permute-done.24 = bf16[256,256]{1,0:T(8,128)(2,1)S(1)} collective-permute-done((bf16[256,256]{1,0:T(8,128)(2,1)S(1)}, bf16[256,256]{1,0:T(8,128)(2,1)S(1)}, u32[]{:S(2)}, u32[]{:S(2)}) %collective-permute-start.24) | collective-permute-done | bytes 131104 | tf_op jit(solution)/shard_map/ppermute | solution.py:28
  365.5 1.8 fusion.24
  (149 shorter events, 35.1 us)
Async XLA Ops:
  6.5 8.1 %copy-start.10 = (bf16[2,32,2048]{2,1,0:T(8,128)(2,1)S(1)}, bf16[2,32,2048]{2,1,0:T(8,128)(2,1)}, u32[]{:S(2)}) copy-start(bf16[2,32,2048]{2,1,0:T(8,128)(2,1)} %param.14) | copy-start | bytes 786436
  6.5 9.1 %copy-start.17 = (s32[256]{0:T(256)S(1)}, s32[256]{0:T(256)}, u32[]{:S(2)}) copy-start(s32[256]{0:T(256)} %param.24) | copy-start | bytes 3076
  6.5 171.1 %all-gather.4.cloned.1.call-start = ((), (), s32[]{:S(2)}) async-start(), calls=%async_computation.1 | async-start | bytes 6684672 | tf_op jit(solution)/shard_map/all_gather | solution.py:284
  8.0 5.0 %collective-permute-start.3 = (bf16[32,8,128]{2,1,0:T(8,128)(2,1)S(1)}, bf16[32,8,128]{2,1,0:T(8,128)(2,1)S(1)}, u32[]{:S(2)}, u32[]{:S(2)}) collective-permute-start(bf16[32,8,128]{2,1,0:T(8,128)(2,1)S(1)} %bitcast.229), channel_id=1, source_target_pairs={{0,1},{1,0},{2,3},{3,2},{4,5},{5,4},{6,7},{7,6},{8,9},{9,8},{10,11... | collective-permute-start | bytes 196616 | tf_op jit(solution)/shard_map/ppermute | solution.py:28
  8.5 6.1 %collective-permute-start.2 = (bf16[32,2048]{1,0:T(8,128)(2,1)S(1)}, bf16[32,2048]{1,0:T(8,128)(2,1)S(1)}, u32[]{:S(2)}, u32[]{:S(2)}) collective-permute-start(bf16[32,2048]{1,0:T(8,128)(2,1)S(1)} %get-tuple-element.39), channel_id=1, source_target_pairs={{0,1},{1,0},{2,3},{3,2},{4,5},{5,4},{6,7},{7,6},{8,9},{9,8},{10,11... | collective-permute-start | bytes 393224 | tf_op jit(solution)/shard_map/ppermute | solution.py:28
  15.5 310.2 %all-gather.8.cloned.1.call-start = ((), (), s32[]{:S(2)}) async-start(), calls=%async_computation.3 | async-start | bytes 1114112 | tf_op jit(solution)/shard_map/all_gather | solution.py:362
  29.4 1.3 copy-start.3
  30.8 2.7 collective-permute-start.19
  34.9 15.9 %collective-permute-start.20 = (bf16[4,256,256]{2,1,0:T(8,128)(2,1)S(1)}, bf16[4,256,256]{2,1,0:T(8,128)(2,1)S(1)}, u32[]{:S(2)}, u32[]{:S(2)}) collective-permute-start(bf16[4,256,256]{2,1,0:T(8,128)(2,1)S(1)} %dynamic-slice_bitcast_fusion.1), channel_id=1, source_target_pairs={{0,4},{2,6},{4,0},{6,2},{8,12},{10,14},{12,8},{14,10},{16,20},{18,... | collective-permute-start | bytes 1572872 | tf_op jit(solution)/shard_map/ppermute | solution.py:62
  36.6 50.4 %copy-start.8 = (bf16[2048,256]{1,0:T(8,128)(2,1)S(1)}, bf16[2048,256]{1,0:T(8,128)(2,1)}, u32[]{:S(2)}) copy-start(bf16[2048,256]{1,0:T(8,128)(2,1)} %param.22) | copy-start | bytes 3145732
  50.9 19.0 %collective-permute-start.21 = (bf16[2,256,256]{2,1,0:T(8,128)(2,1)S(1)}, bf16[2,256,256]{2,1,0:T(8,128)(2,1)S(1)}, u32[]{:S(2)}, u32[]{:S(2)}) collective-permute-start(bf16[2,256,256]{2,1,0:T(8,128)(2,1)S(1)} %dynamic-slice_bitcast_fusion.2), channel_id=1, source_target_pairs={{0,8},{2,10},{4,12},{6,14},{8,0},{10,2},{12,4},{14,6},{16,24},{18,... | collective-permute-start | bytes 786440 | tf_op jit(solution)/shard_map/ppermute | solution.py:62
  70.0 11.8 %collective-permute-start.22 = (bf16[1,256,256]{2,1,0:T(8,128)(2,1)S(1)}, bf16[1,256,256]{2,1,0:T(8,128)(2,1)S(1)}, u32[]{:S(2)}, u32[]{:S(2)}) collective-permute-start(bf16[1,256,256]{2,1,0:T(8,128)(2,1)S(1)} %constant_dynamic-slice_fusion.4), channel_id=1, source_target_pairs={{0,16},{2,18},{4,20},{6,22},{8,24},{10,26},{12,28},{14,30},{16,0},... | collective-permute-start | bytes 393224 | tf_op jit(solution)/shard_map/ppermute | solution.py:62
  82.0 4.3 %collective-permute-start.23 = (bf16[256,128]{1,0:T(8,128)(2,1)S(1)}, bf16[256,128]{1,0:T(8,128)(2,1)S(1)}, u32[]{:S(2)}, u32[]{:S(2)}) collective-permute-start(bf16[256,128]{1,0:T(8,128)(2,1)S(1)} %bitcast.230), channel_id=1, source_target_pairs={{0,1},{1,0},{2,3},{3,2},{4,5},{5,4},{6,7},{7,6},{8,9},{9,8},{10,11... | collective-permute-start | bytes 196616 | tf_op jit(solution)/shard_map/ppermute | solution.py:28
  87.0 251.8 %all-gather.6.cloned.1.call-start = ((), (), s32[]{:S(2)}) async-start(), calls=%async_computation.2 | async-start | bytes 17825792 | tf_op jit(solution)/shard_map/all_gather | solution.py:299
  89.7 12.6 %collective-permute-start.17 = (bf16[2048,128]{1,0:T(8,128)(2,1)S(1)}, bf16[2048,128]{1,0:T(8,128)(2,1)S(1)}, u32[]{:S(2)}, u32[]{:S(2)}) collective-permute-start(bf16[2048,128]{1,0:T(8,128)(2,1)S(1)} %bitcast.220), channel_id=1, source_target_pairs={{0,1},{1,0},{2,3},{3,2},{4,5},{5,4},{6,7},{7,6},{8,9},{9,8},{10,11... | collective-permute-start | bytes 1572872 | tf_op jit(solution)/shard_map/ppermute | solution.py:28
  90.7 13.6 %copy-start.9 = (bf16[256,2048]{1,0:T(8,128)(2,1)S(1)}, bf16[256,2048]{1,0:T(8,128)(2,1)}, u32[]{:S(2)}) copy-start(bf16[256,2048]{1,0:T(8,128)(2,1)} %param.19) | copy-start | bytes 3145732
  103.3 1.7 copy-start.12
  103.3 45.9 %collective-permute-start = (bf16[512,2048]{1,0:T(8,128)(2,1)}, bf16[512,2048]{1,0:T(8,128)(2,1)}, u32[]{:S(2)}, u32[]{:S(2)}) collective-permute-start(bf16[512,2048]{1,0:T(8,128)(2,1)} %param.13), channel_id=1, source_target_pairs={{0,1},{1,0},{2,3},{3,2},{4,5},{5,4},{6,7},{7,6},{8,9},{9,8},{10,11... | collective-permute-start | bytes 6291464 | tf_op jit(solution)/shard_map/ppermute | solution.py:28
  104.9 1.0 copy-start.13
  107.3 7.8 %copy-start.16 = (bf16[2048]{0:T(1024)(128)(2,1)S(1)}, bf16[2048]{0:T(1024)(128)(2,1)}, u32[]{:S(2)}) copy-start(bf16[2048]{0:T(1024)(128)(2,1)} %param.17) | copy-start | bytes 12292
  107.3 8.9 %copy-start.15 = (bf16[2048]{0:T(1024)(128)(2,1)S(1)}, bf16[2048]{0:T(1024)(128)(2,1)}, u32[]{:S(2)}) copy-start(bf16[2048]{0:T(1024)(128)(2,1)} %param.18) | copy-start | bytes 12292
  107.3 65.7 %all-to-all-start = ((bf16[16,256,192]{1,2,0:T(8,128)(2,1)}), bf16[16,256,192]{1,2,0:T(8,128)(2,1)}, u32[]{:S(2)}, u32[]{:S(2)}) async-start(bf16[16,256,192]{1,2,0:T(8,128)(2,1)} %pad_maximum_fusion.1), calls=%async_computation | async-start | bytes 3145728 | tf_op jit(solution)/shard_map/all_to_all | solution.py:275
  115.1 34.1 %collective-permute-start.1 = (bf16[2048]{0:T(1024)(128)(2,1)S(1)}, bf16[2048]{0:T(1024)(128)(2,1)S(1)}, u32[]{:S(2)}, u32[]{:S(2)}) collective-permute-start(bf16[2048]{0:T(1024)(128)(2,1)S(1)} %copy-done.16), channel_id=1, source_target_pairs={{0,1},{1,0},{2,3},{3,2},{4,5},{5,4},{6,7},{7,6},{8,9},{9,8},{10,11... | collective-permute-start | bytes 12296 | tf_op jit(solution)/shard_map/ppermute | solution.py:28
  116.1 33.1 %collective-permute-start.18 = (bf16[2048]{0:T(1024)(128)(2,1)S(1)}, bf16[2048]{0:T(1024)(128)(2,1)S(1)}, u32[]{:S(2)}, u32[]{:S(2)}) collective-permute-start(bf16[2048]{0:T(1024)(128)(2,1)S(1)} %copy-done.15), channel_id=1, source_target_pairs={{0,1},{1,0},{2,3},{3,2},{4,5},{5,4},{6,7},{7,6},{8,9},{9,8},{10,11... | collective-permute-start | bytes 12296 | tf_op jit(solution)/shard_map/ppermute | solution.py:28
  151.8 1.4 copy-start
  173.0 2.9 copy-start.1
  174.7 1.2 copy-start.6
  177.7 3.3 copy-start.7
  185.7 6.8 %copy-start.18 = (s32[1,128]{1,0:T(1,128)S(1)}, s32[1,128]{1,0:T(1,128)}, u32[]{:S(2)}) copy-start(s32[1,128]{1,0:T(1,128)} %param.16) | copy-start | bytes 1540
  188.3 22.5 %collective-permute-start.4 = (bf16[1024,192]{0,1:T(8,128)(2,1)}, bf16[1024,192]{0,1:T(8,128)(2,1)S(1)}, u32[]{:S(2)}, u32[]{:S(2)}) collective-permute-start(bf16[1024,192]{0,1:T(8,128)(2,1)} %constant_dynamic-update-slice_fusion), channel_id=1, source_target_pairs={{0,8},{2,10},{4,12},{6,14},{8,0},{10,2},{12,4},{14,6},{16,24},{18,... | collective-permute-start | bytes 1179656 | tf_op jit(solution)/shard_map/ppermute | solution.py:319
  188.3 35.7 %collective-permute-start.5 = (bf16[1024,192]{0,1:T(8,128)(2,1)}, bf16[1024,192]{0,1:T(8,128)(2,1)S(1)}, u32[]{:S(2)}, u32[]{:S(2)}) collective-permute-start(bf16[1024,192]{0,1:T(8,128)(2,1)} %constant_dynamic-update-slice_fusion), channel_id=1, source_target_pairs={{0,16},{2,18},{4,20},{6,22},{8,24},{10,26},{12,28},{14,30},{16,0},... | collective-permute-start | bytes 1179656 | tf_op jit(solution)/shard_map/ppermute | solution.py:319
  188.4 72.9 %collective-permute-start.6 = (bf16[1024,192]{0,1:T(8,128)(2,1)}, bf16[1024,192]{0,1:T(8,128)(2,1)}, u32[]{:S(2)}, u32[]{:S(2)}) collective-permute-start(bf16[1024,192]{0,1:T(8,128)(2,1)} %constant_dynamic-update-slice_fusion), channel_id=1, source_target_pairs={{0,24},{2,26},{4,28},{6,30},{8,16},{10,18},{12,20},{14,22},{16,8},... | collective-permute-start | bytes 1179656 | tf_op jit(solution)/shard_map/ppermute | solution.py:319
  192.5 1.2 collective-permute-start.7
  192.6 3.6 collective-permute-start.8
  193.7 3.0 collective-permute-start.9
  285.6 29.0 %copy-start.2 = (bf16[512,2048]{1,0:T(8,128)(2,1)S(1)}, bf16[512,2048]{1,0:T(8,128)(2,1)}, u32[]{:S(2)}) copy-start(bf16[512,2048]{1,0:T(8,128)(2,1)} %copy-done) | copy-start | bytes 6291460
  287.4 29.6 %copy-start.5 = (bf16[512,512]{1,0:T(8,128)(2,1)}, bf16[512,512]{1,0:T(8,128)(2,1)S(1)}, u32[]{:S(2)}) copy-start(bf16[512,512]{1,0:T(8,128)(2,1)S(1)} %get-tuple-element.26.refs_0_) | copy-start | bytes 1572868
  287.4 5.1 %collective-permute-start.10 = (bf16[512,512]{1,0:T(8,128)(2,1)S(1)}, bf16[512,512]{1,0:T(8,128)(2,1)S(1)}, u32[]{:S(2)}, u32[]{:S(2)}) collective-permute-start(bf16[512,512]{1,0:T(8,128)(2,1)S(1)} %get-tuple-element.25), channel_id=1, source_target_pairs={{0,2},{2,0},{4,6},{6,4},{8,10},{10,8},{12,14},{14,12},{16,18},{18,... | collective-permute-start | bytes 1572872 | tf_op jit(solution)/shard_map/ppermute | solution.py:344
  287.5 15.0 %collective-permute-start.11 = (bf16[512,512]{1,0:T(8,128)(2,1)S(1)}, bf16[512,512]{1,0:T(8,128)(2,1)}, u32[]{:S(2)}, u32[]{:S(2)}) collective-permute-start(bf16[512,512]{1,0:T(8,128)(2,1)S(1)} %get-tuple-element.24), channel_id=1, source_target_pairs={{0,4},{2,6},{4,0},{6,2},{8,12},{10,14},{12,8},{14,10},{16,20},{18,... | collective-permute-start | bytes 1572872 | tf_op jit(solution)/shard_map/ppermute | solution.py:344
  287.6 25.0 %collective-permute-start.12 = (bf16[512,512]{1,0:T(8,128)(2,1)S(1)}, bf16[512,512]{1,0:T(8,128)(2,1)}, u32[]{:S(2)}, u32[]{:S(2)}) collective-permute-start(bf16[512,512]{1,0:T(8,128)(2,1)S(1)} %get-tuple-element.23), channel_id=1, source_target_pairs={{0,6},{2,4},{4,2},{6,0},{8,14},{10,12},{12,10},{14,8},{16,22},{18,... | collective-permute-start | bytes 1572872 | tf_op jit(solution)/shard_map/ppermute | solution.py:344
  290.6 35.2 %collective-permute-start.13 = (bf16[512,512]{1,0:T(8,128)(2,1)S(1)}, bf16[512,512]{1,0:T(8,128)(2,1)}, u32[]{:S(2)}, u32[]{:S(2)}) collective-permute-start(bf16[512,512]{1,0:T(8,128)(2,1)S(1)} %get-tuple-element.26.refs_0_), channel_id=1, source_target_pairs={{0,1},{1,0},{2,3},{3,2},{4,5},{5,4},{6,7},{7,6},{8,9},{9,8},{10,11... | collective-permute-start | bytes 1572872 | tf_op jit(solution)/shard_map/ppermute | solution.py:28
  292.5 24.5 %copy-start.11 = (bf16[512,512]{1,0:T(8,128)(2,1)}, bf16[512,512]{1,0:T(8,128)(2,1)S(1)}, u32[]{:S(2)}) copy-start(bf16[512,512]{1,0:T(8,128)(2,1)S(1)} %collective-permute-done.10.refs_1_) | copy-start | bytes 1572868
  292.5 33.2 %collective-permute-start.14 = (bf16[512,512]{1,0:T(8,128)(2,1)S(1)}, bf16[512,512]{1,0:T(8,128)(2,1)}, u32[]{:S(2)}, u32[]{:S(2)}) collective-permute-start(bf16[512,512]{1,0:T(8,128)(2,1)S(1)} %collective-permute-done.10.refs_1_), channel_id=1, source_target_pairs={{0,1},{1,0},{2,3},{3,2},{4,5},{5,4},{6,7},{7,6},{8,9},{9,8},{10,11... | collective-permute-start | bytes 1572872 | tf_op jit(solution)/shard_map/ppermute | solution.py:28
  302.5 25.5 %collective-permute-start.15 = (bf16[512,512]{1,0:T(8,128)(2,1)}, bf16[512,512]{1,0:T(8,128)(2,1)}, u32[]{:S(2)}, u32[]{:S(2)}) collective-permute-start(bf16[512,512]{1,0:T(8,128)(2,1)} %collective-permute-done.11.refs_2_), channel_id=1, source_target_pairs={{0,1},{1,0},{2,3},{3,2},{4,5},{5,4},{6,7},{7,6},{8,9},{9,8},{10,11... | collective-permute-start | bytes 1572872 | tf_op jit(solution)/shard_map/ppermute | solution.py:28
  312.6 26.1 %collective-permute-start.16 = (bf16[512,512]{1,0:T(8,128)(2,1)}, bf16[512,512]{1,0:T(8,128)(2,1)}, u32[]{:S(2)}, u32[]{:S(2)}) collective-permute-start(bf16[512,512]{1,0:T(8,128)(2,1)} %collective-permute-done.12.refs_3_), channel_id=1, source_target_pairs={{0,1},{1,0},{2,3},{3,2},{4,5},{5,4},{6,7},{7,6},{8,9},{9,8},{10,11... | collective-permute-start | bytes 1572872 | tf_op jit(solution)/shard_map/ppermute | solution.py:28
  338.8 26.7 %copy-start.14 = (f32[256,256]{1,0:T(8,128)S(1)}, f32[256,256]{1,0:T(8,128)}, u32[]{:S(2)}) copy-start(f32[256,256]{1,0:T(8,128)} %param.25) | copy-start | bytes 786436
  357.7 3.6 collective-permute-start.25
  360.5 5.0 %collective-permute-start.24 = (bf16[256,256]{1,0:T(8,128)(2,1)S(1)}, bf16[256,256]{1,0:T(8,128)(2,1)S(1)}, u32[]{:S(2)}, u32[]{:S(2)}) collective-permute-start(bf16[256,256]{1,0:T(8,128)(2,1)S(1)} %fusion.25), channel_id=1, source_target_pairs={{0,1},{1,0},{2,3},{3,2},{4,5},{5,4},{6,7},{7,6},{8,9},{9,8},{10,11... | collective-permute-start | bytes 393224 | tf_op jit(solution)/shard_map/ppermute | solution.py:28
  (1 other events, 0.8 us)
Sparse Core Ops, SparseCore 0:
  15.6 67.9 all-gather.3
  87.1 43.2 all-gather.7
  132.6 166.6 all-gather.5
where the time goes:
time: 375 us; the launch traced here: 374 us
  waiting for transfers between devices  218 us (58%)
  local copies, waits for them, and re-layouts  40 us (11%)
  Pallas kernels  39 us (10%)
  starting transfers between devices  35.3 us (9%)
  other arithmetic  21.7 us (6%)
  between operations  14.4 us (4%)
  matrix products  5.53 us (1%)
    ppermute x13, waiting for transfers between devices, swap_tp(): return lax.ppermute(x, 'tp', [(0, 1), (1, 0)])  68.5 us
    ppermute x3, waiting for transfers between devices, on_device(): lax.ppermute(piece, 'patch', xor_pairs(n_p, k * kv_here))  64.5 us
    ppermute x4, waiting for transfers between devices, reduce_patch(): x = keep + lax.ppermute(send, 'patch', xor_pairs(n, flip))  43.5 us
    all_to_all x1, waiting for transfers between devices, on_device(): lax.all_to_all(send, 'patch', 0, 0, tiled=True).reshape(D, send.shape[2])  19.8 us
    ppermute x3, waiting for transfers between devices, on_device(): lax.ppermute(attended[j], 'patch', xor_pairs(n_p, j))  18.1 us
    pallas_call x1, Pallas kernels, finish(): pl.pallas_call(finish_body, grid_spec=pltpu.PrefetchScalarGridSpec(num_sc...  17.9 us
    ppermute x13, starting transfers between devices, swap_tp(): return lax.ppermute(x, 'tp', [(0, 1), (1, 0)])  15.3 us
    gather x1, local copies, waits for them, and re-layouts, on_device(): jnp.take(unembed, jnp.clip(local, 0, rows_dev - 1), axis=0)  13.3 us
  transfers between devices with their start and end apart: 30, of which 22 were waited for; matrix products, arithmetic and copies ran while one was open for 15% of the time, Pallas kernels for 6%

commit v1 on v0

--- a/solution.py
+++ b/solution.py
@@ -62,6 +62,20 @@
         x = keep + lax.ppermute(send, "patch", xor_pairs(n, flip))
         flip *= 2
     return x[0]
+
+
+def gather_patch(x):
+    n = lax.axis_size("patch")
+    me = lax.axis_index("patch")
+    got = x[None]
+    flip = n // 2
+    while flip:
+        other = lax.ppermute(got, "patch", xor_pairs(n, flip))
+        low = (me // flip) % 2 == 0
+        got = jnp.stack([jnp.where(low, got, other), jnp.where(low, other, got)], axis=1)
+        got = got.reshape((-1,) + x.shape)
+        flip //= 2
+    return got
 
 
 def rope_angles(first, count):
@@ -123,14 +137,12 @@
     )(q, k, v, masks)
 
 
-def splice_body(place_ref, corrupt_a, corrupt_b, clean_a, clean_b, late_ref, code_ref, o_ref):
+def splice_body(place_ref, corrupt_a, corrupt_b, clean_a, clean_b, code_ref, o_ref):
     code = code_ref[...]
     code = jnp.concatenate([code, code], axis=1)
     corrupt = jnp.concatenate([corrupt_a[...], corrupt_b[...]], axis=1).astype(jnp.float32)
     clean = jnp.concatenate([clean_a[...], clean_b[...]], axis=1).astype(jnp.float32)
-    rows = jnp.where(code == 1, clean, corrupt)
-    rows = jnp.where(code == 2, late_ref[...].astype(jnp.float32), rows)
-    o_ref[...] = rows.astype(jnp.bfloat16)
+    o_ref[...] = jnp.where(code == 1, clean, corrupt).astype(jnp.bfloat16)
 
 
 def splice(place, corrupt, clean, code, columns):
@@ -149,36 +161,33 @@
                 pl.BlockSpec((tokens, sub), lambda i, s: (0, lane(2 * i + 1, s))),
                 pl.BlockSpec((tokens, sub), lambda i, s: (0, lane(2 * i, s))),
                 pl.BlockSpec((tokens, sub), lambda i, s: (0, lane(2 * i + 1, s))),
-                pl.BlockSpec((tokens, 2 * sub), lambda i, s: (0, D // (2 * sub) + i)),
                 pl.BlockSpec((tokens, sub), lambda i, s: (0, 0)),
             ],
             out_specs=pl.BlockSpec((tokens, 2 * sub), lambda i, s: (0, i)),
         ),
         out_shape=jax.ShapeDtypeStruct((tokens, columns), jnp.bfloat16),
         name="splice",
-    )(place, corrupt, corrupt, clean, clean, clean, code)
+    )(place, corrupt, corrupt, clean, clean, code)
 
 
 def finish_body(place_ref, *refs):
     heads = [refs[:4], refs[4:8]]
-    w_ref, base_ref, code_ref, gain_ref, score_ref = refs[8:13]
-    o_ref, sum_ref = refs[13:]
+    w_ref, base_ref, gain_ref, score_ref = refs[8:12]
+    o_ref, sum_ref = refs[12:]
     step = pl.program_id(0)
     rows = heads[0][0].shape[1]
-    code = code_ref[...]
-    code = jnp.concatenate([code, code], axis=1)
-    base = base_ref[...].astype(jnp.float32)
-    residual = base
+    residual = base_ref[...].astype(jnp.float32)
     for half in range(2):
         term = None
         for slot in range(4):
             at = pl.multiple_of((half * 4 + (place_ref[1] ^ slot)) * rows, rows)
             part = jnp.dot(
-                heads[half][slot][...], w_ref[pl.ds(at, rows), :], preferred_element_type=jnp.float32
+                heads[half][slot][...],
+                jnp.concatenate([w_ref[0, pl.ds(at, rows), :], w_ref[1, pl.ds(at, rows), :]], axis=1),
+                preferred_element_type=jnp.float32,
             )
             term = part if term is None else term + part
         residual = residual + term.astype(jnp.bfloat16).astype(jnp.float32)
-    residual = jnp.where(code == 2, base, residual)
     final = (residual * gain_ref[...].astype(jnp.float32)).astype(jnp.bfloat16)
     score = jnp.concatenate([score_ref[0], score_ref[1]], axis=1)
     logits = lax.dot_general(
@@ -203,9 +212,9 @@
         sum_ref[...] = jnp.broadcast_to(total, sum_ref.shape)
 
 
-def finish(place, heads, weights, base, code, gain, score):
+def finish(place, heads, weights, base, gain, score):
     tokens, block = heads[0].shape
-    columns = weights.shape[1]
+    columns = base.shape[1]
     scored, sub = score.shape[1:]
 
     whole = pl.BlockSpec((tokens, block), lambda i, s: (0, 0))
@@ -216,9 +225,8 @@
             grid=(columns // (2 * sub),),
             in_specs=[whole] * 8
             + [
-                pl.BlockSpec((weights.shape[0], 2 * sub), lambda i, s: (0, i)),
+                pl.BlockSpec((2, weights.shape[1], sub), lambda i, s: (i, 0, 0)),
                 pl.BlockSpec((tokens, 2 * sub), lambda i, s: (0, i)),
-                pl.BlockSpec((tokens, sub), lambda i, s: (0, 0)),
                 pl.BlockSpec((1, 2 * sub), lambda i, s: (0, i)),
                 pl.BlockSpec((2, scored, sub), lambda i, s: (i, 0, 0)),
             ],
@@ -232,7 +240,7 @@
             jax.ShapeDtypeStruct((tokens, sub), jnp.float32),
         ],
         name="finish",
-    )(place, *heads, weights, base, code, gain, score)
+    )(place, *heads, weights, base, gain, score)
 
 
 def on_device(
@@ -281,10 +289,7 @@
         resid_clean[1].reshape(rows_here, slices_t, n_t, sub).transpose(2, 0, 1, 3)
     )
     late_rows_here = jnp.concatenate(late_parts, axis=1).reshape(rows_here, n_p * sub)
-    both_sites = lax.all_gather(
-        jnp.concatenate([clean_rows, late_rows_here], axis=1), "patch", axis=0, tiled=True
-    )
-    clean_full = both_sites[:, :D]
+    clean_full = lax.all_gather(clean_rows, "patch", axis=0, tiled=True)
     gain_full = jnp.concatenate(over_tp(norm_gain)).astype(f32)
     final_full = jnp.concatenate(over_tp(final_gain)).astype(f32)
 
@@ -296,7 +301,11 @@
         )
     else:
         out_rows = jnp.concatenate(exchange_tp(out_block), axis=0)
-    out_cols = lax.all_gather(out_rows, "patch", axis=1, tiled=True)
+    if fused:
+        out_cols = lax.all_gather(out_rows, "patch", axis=0, tiled=True)
+        out_cols = out_cols.reshape((n_p,) + out_rows.shape)
+    else:
+        out_cols = lax.all_gather(out_rows, "patch", axis=1, tiled=True)
 
     def project(rows):
         rows = rows.astype(f32)
@@ -366,13 +375,33 @@
     final_own = lax.dynamic_index_in_dim(
         final_full.reshape(n_p, n_t, sub), me_t, 1, keepdims=False
     ).reshape(1, n_p * sub)
+
+    late_f = late_rows_here.astype(f32)
+    late_final = (late_f * final_own).astype(bf16).reshape(rows_here, n_p, sub)
+    late_logits = jnp.einsum("rpj,psj->rs", late_final, score, preferred_element_type=f32)
+    late_squares = jnp.broadcast_to(
+        jnp.sum(late_f * late_f, axis=1, keepdims=True), (rows_here, HD)
+    )
+    packed = jnp.concatenate([late_logits, late_squares], axis=1)
+    packed = packed + swap_tp(packed) if n_t == 2 else lax.psum(packed, "tp")
+    packed = gather_patch(packed).reshape(tokens, scored + HD)
+    packed = lax.dynamic_slice_in_dim(packed, me_t * share, share, 0)
+    late_total, late_sum = packed[:, :scored], packed[:, scored]
+    is_late = row_mask & (patch_level[0] == 1)
+    is_late = lax.dynamic_slice_in_dim(is_late, me_t * share, share, 0)
+
+    def scored_shift(total, square_sum):
+        total = jnp.where(is_late[:, None], late_total, total)
+        scaling = lax.rsqrt(jnp.where(is_late, late_sum, square_sum) / D + EPSILON)
+        return (total * scaling[:, None] - base_logits)[None]
+
     if fused:
         heads = mine + [swap_tp(x) for x in mine]
         code = jnp.where(row_mask, 1 + patch_level[0], 0)
         code = jnp.broadcast_to(code[:, None], (tokens, sub))
         place = jnp.stack([me_t, me_b]).astype(jnp.int32)
-        base = splice(place, corrupt_full, both_sites, code, n_p * sub)
-        parts = finish(place, heads, out_cols, base, code, final_own, score)
+        base = splice(place, corrupt_full, clean_full, code, n_p * sub)
+        parts = finish(place, heads, out_cols, base, final_own, score)
         logits, squares = (x.reshape(n_t, share, -1) for x in parts)
 
         def halves(x):
@@ -385,8 +414,7 @@
         squares_keep, squares_send = halves(squares[:, :, 0])
         square_sum = squares_keep + swap_tp(squares_send)
         total = logits_keep + swap_tp(logits_send.astype(bf16)).astype(f32)
-        scaling = lax.rsqrt(square_sum / D + EPSILON)[:, None]
-        return (total * scaling - base_logits)[None]
+        return scored_shift(total, square_sum)
 
     def in_order(slots):
         stacked = jnp.stack(slots)
@@ -401,7 +429,6 @@
     by_slot = [over_tp(x) for x in mine]
     rows_t = w_out.shape[0]
     early_rows = jnp.tile(early_here[0], PROMPTS)[:, None] > 0.5
-    late_rows = (row_mask & (patch_level[0] == 1))[:, None]
 
     def own_features(x):
         own = lax.dynamic_index_in_dim(x.reshape(tokens, n_p, n_t, sub), me_t, 2, keepdims=False)
@@ -416,14 +443,12 @@
             preferred_element_type=f32,
         )
         residual = residual + term.astype(bf16).astype(f32)
-    residual = jnp.where(late_rows, both_sites[:, D:].astype(f32), residual)
     squares = jnp.sum(residual * residual, axis=1)
     final_block = (residual * final_own).astype(bf16).reshape(tokens, n_p, sub)
     logits = jnp.einsum("rpj,psj->rs", final_block, score, preferred_element_type=f32)
     total = sum(exchange_tp(logits.reshape(n_t, share, -1)))
     square_sum = sum(exchange_tp(squares.reshape(n_t, share)))
-    scaling = lax.rsqrt(square_sum / D + EPSILON)[:, None]
-    return (total * scaling - base_logits)[None]
+    return scored_shift(total, square_sum)
 
 
 def solution(mesh):

time: 375 us -> 385 us (1.027)
  the two profiles are of different devices: /device:TPU:20 before, /device:TPU:0 now
where the time goes in v1:
time: 385 us; the launch traced here: 383 us
  waiting for transfers between devices  219 us (57%)
  starting transfers between devices  43.4 us (11%)
  Pallas kernels  38.3 us (10%)
  local copies, waits for them, and re-layouts  36.5 us (9%)
  other arithmetic  24.8 us (6%)
  between operations  14.5 us (4%)
  matrix products  6.35 us (2%)
    ppermute x14, waiting for transfers between devices, swap_tp(): return lax.ppermute(x, 'tp', [(0, 1), (1, 0)])  56.3 us
    ppermute x3, waiting for transfers between devices, on_device(): lax.ppermute(piece, 'patch', xor_pairs(n_p, k * kv_here))  44.3 us
    ppermute x3, waiting for transfers between devices, on_device(): lax.ppermute(attended[j], 'patch', xor_pairs(n_p, j))  41.3 us
    all_gather x1, waiting for transfers between devices, on_device(): out_cols = lax.all_gather(out_rows, 'patch', axis=0, tiled=True)  34.8 us
    ppermute x4, waiting for transfers between devices, reduce_patch(): x = keep + lax.ppermute(send, 'patch', xor_pairs(n, flip))  25.3 us
    pallas_call x1, Pallas kernels, finish(): pl.pallas_call(finish_body, grid_spec=pltpu.PrefetchScalarGridSpec(num_sc...  17.7 us
    ppermute x14, starting transfers between devices, swap_tp(): return lax.ppermute(x, 'tp', [(0, 1), (1, 0)])  16.3 us
    gather x1, local copies, waits for them, and re-layouts, on_device(): jnp.take(unembed, jnp.clip(local, 0, rows_dev - 1), axis=0)  13.4 us
  transfers between devices with their start and end apart: 35, of which 20 were waited for; matrix products, arithmetic and copies ran while one was open for 11% of the time, Pallas kernels for 5%

profile of v1, /device:TPU:0, one launch (start us, length us, event | category | flops | bytes accessed | tf_op | source)
XLA Modules:
  0.0 383.1 jit_solution(1362294866642086738)
XLA Ops:
  7.2 13.4 %gather_fusion = bf16[256,4096]{1,0:T(8,128)(2,1)S(1)} fusion(bf16[4008,4096]{1,0:T(8,128)(2,1)} %param.23, s32[1024]{0:T(1024)S(1)} %pad_clamp_fusion), kind=kCustom, calls=%fused_computation | custom fusion | bytes 4195328 | tf_op jit(solution)/shard_map/jit(_take)/gather | solution.py:360
  23.0 2.3 collective-permute-done.2
  26.7 2.6 collective-permute-start.3
  29.3 12.2 %collective-permute-done.3 = bf16[4,256,256]{2,1,0:T(8,128)(2,1)S(1)} collective-permute-done((bf16[4,256,256]{2,1,0:T(8,128)(2,1)S(1)}, bf16[4,256,256]{2,1,0:T(8,128)(2,1)S(1)}, u32[]{:S(2)}, u32[]{:S(2)}) %collective-permute-start.3) | collective-permute-done | bytes 524320 | tf_op jit(solution)/shard_map/ppermute | solution.py:62
  41.6 2.2 collective-permute-start.4
  43.8 5.7 %collective-permute-done.4 = bf16[2,256,256]{2,1,0:T(8,128)(2,1)S(1)} collective-permute-done((bf16[2,256,256]{2,1,0:T(8,128)(2,1)S(1)}, bf16[2,256,256]{2,1,0:T(8,128)(2,1)S(1)}, u32[]{:S(2)}, u32[]{:S(2)}) %collective-permute-start.4) | collective-permute-done | bytes 262176 | tf_op jit(solution)/shard_map/ppermute | solution.py:62
  49.6 2.8 collective-permute-start.5
  52.5 5.0 %collective-permute-done.5 = bf16[1,256,256]{2,1,0:T(8,128)(2,1)S(1)} collective-permute-done((bf16[1,256,256]{2,1,0:T(8,128)(2,1)S(1)}, bf16[1,256,256]{2,1,0:T(8,128)(2,1)S(1)}, u32[]{:S(2)}, u32[]{:S(2)}) %collective-permute-start.5) | collective-permute-done | bytes 131104 | tf_op jit(solution)/shard_map/ppermute | solution.py:62
  57.8 1.5 collective-permute-start.6
  59.3 2.9 collective-permute-done.6
  63.0 1.6 collective-permute-start.14
  64.5 3.6 collective-permute-done.14
  70.0 1.7 collective-permute-start.28
  72.0 7.3 %collective-permute-done.28 = bf16[2048,128]{1,0:T(8,128)(2,1)S(1)} collective-permute-done((bf16[2048,128]{1,0:T(8,128)(2,1)S(1)}, bf16[2048,128]{1,0:T(8,128)(2,1)S(1)}, u32[]{:S(2)}, u32[]{:S(2)}) %collective-permute-start.28) | collective-permute-done | bytes 524320 | tf_op jit(solution)/shard_map/ppermute | solution.py:28
  81.6 1.5 collective-permute-start.19
  83.1 1.7 collective-permute-start.1
  85.2 1.7 collective-permute-start.12
  89.8 5.9 %all-to-all-start = ((bf16[16,256,192]{1,2,0:T(8,128)(2,1)}), bf16[16,256,192]{1,2,0:T(8,128)(2,1)}, u32[]{:S(2)}, u32[]{:S(2)}) async-start(bf16[16,256,192]{1,2,0:T(8,128)(2,1)} %pad_maximum_fusion.1), calls=%async_computation | async-start | bytes 3145728 | tf_op jit(solution)/shard_map/all_to_all | solution.py:283
  97.1 1.6 collective-permute-start.20
  100.1 33.9 %collective-permute-done = bf16[32,8,128]{2,0,1:T(8,128)(2,1)S(1)} collective-permute-done((bf16[32,8,128]{2,0,1:T(8,128)(2,1)S(1)}, bf16[32,8,128]{2,0,1:T(8,128)(2,1)S(1)}, u32[]{:S(2)}, u32[]{:S(2)}) %collective-permute-start) | collective-permute-done | bytes 65568 | tf_op jit(solution)/shard_map/ppermute | solution.py:28
  134.2 2.5 broadcast_select_fusion.1
  139.1 1.6 convolution_bitcast_fusion
  140.8 1.6 collective-permute-start.7
  142.5 1.7 copy.104
  144.9 1.8 collective-permute-start.8
  146.7 1.7 fusion.8
  148.5 5.1 %collective-permute-done.8 = f32[1,32,384]{2,1,0:T(8,128)S(1)} collective-permute-done((f32[1,32,384]{2,1,0:T(8,128)S(1)}, f32[1,32,384]{2,1,0:T(8,128)S(1)}, u32[]{:S(2)}, u32[]{:S(2)}) %collective-permute-start.8) | collective-permute-done | bytes 49184 | tf_op jit(solution)/shard_map/ppermute | solution.py:73
  154.1 12.2 %all-gather.6.cloned.1.call-done.clean_a.clean_b = bf16[512,4096]{1,0:T(8,128)(2,1)} async-done(((bf16[32,4096]{1,0:T(8,128)(2,1)}), bf16[512,4096]{1,0:T(8,128)(2,1)}) %all-gather.6.cloned.1.call-update) | async-done | bytes 4194320 | tf_op jit(solution)/shard_map/all_gather | solution.py:292
  166.3 3.2 fusion.3
  169.7 3.0 fusion.6
  174.6 1.4 collective-permute-start.16
  176.0 1.8 collective-permute-start.17
  180.0 24.7 %collective-permute-done.15 = bf16[1024,192]{0,1:T(8,128)(2,1)S(1)} collective-permute-done((bf16[1024,192]{0,1:T(8,128)(2,1)S(1)}, bf16[1024,192]{0,1:T(8,128)(2,1)S(1)}, u32[]{:S(2)}, u32[]{:S(2)}) %collective-permute-start.15) | collective-permute-done | bytes 393248 | tf_op jit(solution)/shard_map/ppermute | solution.py:328
  204.7 13.6 %collective-permute-done.16 = bf16[1024,192]{0,1:T(8,128)(2,1)S(1)} collective-permute-done((bf16[1024,192]{0,1:T(8,128)(2,1)S(1)}, bf16[1024,192]{0,1:T(8,128)(2,1)S(1)}, u32[]{:S(2)}, u32[]{:S(2)}) %collective-permute-start.16) | collective-permute-done | bytes 393248 | tf_op jit(solution)/shard_map/ppermute | solution.py:328
  218.2 6.0 %collective-permute-done.17 = bf16[1024,192]{0,1:T(8,128)(2,1)S(1)} collective-permute-done((bf16[1024,192]{0,1:T(8,128)(2,1)S(1)}, bf16[1024,192]{0,1:T(8,128)(2,1)S(1)}, u32[]{:S(2)}, u32[]{:S(2)}) %collective-permute-start.17) | collective-permute-done | bytes 393248 | tf_op jit(solution)/shard_map/ppermute | solution.py:328
  227.0 1.8 copy.90.k_ref
  234.3 13.3 %attend.1 = bf16[4,512,512]{2,1,0:T(8,128)(2,1)} custom-call(bf16[4,2,4,128,128]{4,3,2,1,0:T(8,128)(2,1)} %bitcast.232, bf16[2,4,128,128]{3,2,1,0:T(8,128)(2,1)} %copy.90.k_ref, bf16[2,4,128,128]{3,2,1,0:T(8,128)(2,1)} %copy.91.v_ref, f32[4,128,128]{2,1,0:T(8,128)} %broadcast_in_dim.83.m_ref), custom_call_target="tpu_custom_call" | custom-call | tf_op jit(solution)/shard_map/attend/pallas_call | solution.py:125
  247.6 2.7 slice_bitcast_fusion
  256.4 20.3 %collective-permute-done.22.refs_2_ = bf16[512,512]{1,0:T(8,128)(2,1)} collective-permute-done((bf16[512,512]{1,0:T(8,128)(2,1)}, bf16[512,512]{1,0:T(8,128)(2,1)}, u32[]{:S(2)}, u32[]{:S(2)}) %collective-permute-start.22) | collective-permute-done | bytes 524320 | tf_op jit(solution)/shard_map/ppermute | solution.py:353
  277.6 21.0 %collective-permute-done.23.refs_3_ = bf16[512,512]{1,0:T(8,128)(2,1)} collective-permute-done((bf16[512,512]{1,0:T(8,128)(2,1)}, bf16[512,512]{1,0:T(8,128)(2,1)}, u32[]{:S(2)}, u32[]{:S(2)}) %collective-permute-start.23) | collective-permute-done | bytes 524320 | tf_op jit(solution)/shard_map/ppermute | solution.py:353
  299.3 2.4 pad_maximum_fusion.corrupt_a.corrupt_b
  302.9 7.3 %splice.1.refs_9_ = bf16[512,2048]{1,0:T(8,128)(2,1)} custom-call(s32[2]{0:T(128)} %pad_add_fusion.place_ref, bf16[512,4096]{1,0:T(8,128)(2,1)} %pad_maximum_fusion.corrupt_a.corrupt_b, bf16[512,4096]{1,0:T(8,128)(2,1)} %pad_maximum_fusion.corrupt_a.corrupt_b, bf16[512,4096]{1,0:T(8,128)(2,1)} %all-gather.6.cloned.1.call-done.clean_a.clean_b, ...), custom_call_target="tpu_custom_call" | custom-call | tf_op jit(solution)/shard_map/splice/pallas_call | solution.py:154
  310.2 3.1 collective-permute-done.27.refs_7_
  313.3 34.8 %all-gather.8.cloned.1.call-done = bf16[65536,128]{1,0:T(8,128)(2,1)} async-done(((bf16[4096,128]{1,0:T(8,128)(2,1)}), bf16[65536,128]{1,0:T(8,128)(2,1)}) %all-gather.8.cloned.1.call-update) | async-done | bytes 16777232 | tf_op jit(solution)/shard_map/all_gather | solution.py:305
  348.1 17.7 %finish.1 = (f32[512,256]{1,0:T(8,128)}, f32[512,128]{1,0:T(8,128)}) custom-call(s32[2]{0:T(128)} %pad_add_fusion.place_ref, bf16[512,512]{1,0:T(8,128)(2,1)} %copy-done.6, bf16[512,512]{1,0:T(8,128)(2,1)} %copy-done.11, bf16[512,512]{1,0:T(8,128)(2,1)} %collective-permute-done.22.refs_2_, bf16[512,512]{1,0:T(8,128)(2,1)} %collective-permute-done.23.refs_3_, ...), custom_call_target="tpu_custom_call" | custom-call | tf_op jit(solution)/shard_map/finish/pallas_call | solution.py:221
  366.8 1.5 collective-permute-start.30
  370.5 4.3 %collective-permute-done.29 = bf16[256,256]{1,0:T(8,128)(2,1)S(1)} collective-permute-done((bf16[256,256]{1,0:T(8,128)(2,1)S(1)}, bf16[256,256]{1,0:T(8,128)(2,1)S(1)}, u32[]{:S(2)}, u32[]{:S(2)}) %collective-permute-start.29) | collective-permute-done | bytes 131104 | tf_op jit(solution)/shard_map/ppermute | solution.py:28
  374.8 1.8 fusion.25
  (180 shorter events, 43.6 us)
Async XLA Ops:
  6.5 132.6 %all-gather.4.cloned.1.call-start = ((), (), s32[]{:S(2)}) async-start(), calls=%async_computation.1 | async-start | bytes 1114112 | tf_op jit(solution)/shard_map/all_gather | solution.py:371
  22.5 2.9 collective-permute-start.2
  26.7 14.8 %collective-permute-start.3 = (bf16[4,256,256]{2,1,0:T(8,128)(2,1)S(1)}, bf16[4,256,256]{2,1,0:T(8,128)(2,1)S(1)}, u32[]{:S(2)}, u32[]{:S(2)}) collective-permute-start(bf16[4,256,256]{2,1,0:T(8,128)(2,1)S(1)} %dynamic-slice_bitcast_fusion.1), channel_id=1, source_target_pairs={{0,4},{2,6},{4,0},{6,2},{8,12},{10,14},{12,8},{14,10},{16,20},{18,... | collective-permute-start | bytes 1572872 | tf_op jit(solution)/shard_map/ppermute | solution.py:62
  29.3 33.6 %copy-start.10 = (bf16[2,32,2048]{2,1,0:T(8,128)(2,1)S(1)}, bf16[2,32,2048]{2,1,0:T(8,128)(2,1)}, u32[]{:S(2)}) copy-start(bf16[2,32,2048]{2,1,0:T(8,128)(2,1)} %param.14) | copy-start | bytes 786436
  41.6 7.9 %collective-permute-start.4 = (bf16[2,256,256]{2,1,0:T(8,128)(2,1)S(1)}, bf16[2,256,256]{2,1,0:T(8,128)(2,1)S(1)}, u32[]{:S(2)}, u32[]{:S(2)}) collective-permute-start(bf16[2,256,256]{2,1,0:T(8,128)(2,1)S(1)} %dynamic-slice_bitcast_fusion.2), channel_id=1, source_target_pairs={{0,8},{2,10},{4,12},{6,14},{8,0},{10,2},{12,4},{14,6},{16,24},{18,... | collective-permute-start | bytes 786440 | tf_op jit(solution)/shard_map/ppermute | solution.py:62
  43.8 25.1 %copy-start.8 = (bf16[2048,256]{1,0:T(8,128)(2,1)S(1)}, bf16[2048,256]{1,0:T(8,128)(2,1)}, u32[]{:S(2)}) copy-start(bf16[2048,256]{1,0:T(8,128)(2,1)} %param.22) | copy-start | bytes 3145732
  49.6 7.9 %collective-permute-start.5 = (bf16[1,256,256]{2,1,0:T(8,128)(2,1)S(1)}, bf16[1,256,256]{2,1,0:T(8,128)(2,1)S(1)}, u32[]{:S(2)}, u32[]{:S(2)}) collective-permute-start(bf16[1,256,256]{2,1,0:T(8,128)(2,1)S(1)} %constant_dynamic-slice_fusion.10), channel_id=1, source_target_pairs={{0,16},{2,18},{4,20},{6,22},{8,24},{10,26},{12,28},{14,30},{16,0},... | collective-permute-start | bytes 393224 | tf_op jit(solution)/shard_map/ppermute | solution.py:62
  57.8 4.4 %collective-permute-start.6 = (bf16[256,128]{1,0:T(8,128)(2,1)S(1)}, bf16[256,128]{1,0:T(8,128)(2,1)S(1)}, u32[]{:S(2)}, u32[]{:S(2)}) collective-permute-start(bf16[256,128]{1,0:T(8,128)(2,1)S(1)} %bitcast.266), channel_id=1, source_target_pairs={{0,1},{1,0},{2,3},{3,2},{4,5},{5,4},{6,7},{7,6},{8,9},{9,8},{10,11... | collective-permute-start | bytes 196616 | tf_op jit(solution)/shard_map/ppermute | solution.py:28
  62.9 103.4 %all-gather.6.cloned.1.call-start = ((), (), s32[]{:S(2)}) async-start(), calls=%async_computation.2 | async-start | bytes 4456448 | tf_op jit(solution)/shard_map/all_gather | solution.py:292
  63.0 5.2 %collective-permute-start.14 = (bf16[32,2048]{1,0:T(8,128)(2,1)S(1)}, bf16[32,2048]{1,0:T(8,128)(2,1)S(1)}, u32[]{:S(2)}, u32[]{:S(2)}) collective-permute-start(bf16[32,2048]{1,0:T(8,128)(2,1)S(1)} %get-tuple-element.45), channel_id=1, source_target_pairs={{0,1},{1,0},{2,3},{3,2},{4,5},{5,4},{6,7},{7,6},{8,9},{9,8},{10,11... | collective-permute-start | bytes 393224 | tf_op jit(solution)/shard_map/ppermute | solution.py:28
  68.9 279.2 %all-gather.8.cloned.1.call-start = ((), (), s32[]{:S(2)}) async-start(), calls=%async_computation.3 | async-start | bytes 17825792 | tf_op jit(solution)/shard_map/all_gather | solution.py:305
  70.0 9.2 %collective-permute-start.28 = (bf16[2048,128]{1,0:T(8,128)(2,1)S(1)}, bf16[2048,128]{1,0:T(8,128)(2,1)S(1)}, u32[]{:S(2)}, u32[]{:S(2)}) collective-permute-start(bf16[2048,128]{1,0:T(8,128)(2,1)S(1)} %bitcast.255), channel_id=1, source_target_pairs={{0,1},{1,0},{2,3},{3,2},{4,5},{5,4},{6,7},{7,6},{8,9},{9,8},{10,11... | collective-permute-start | bytes 1572872 | tf_op jit(solution)/shard_map/ppermute | solution.py:28
  71.7 9.4 %copy-start.19 = (s32[1,128]{1,0:T(1,128)S(1)}, s32[1,128]{1,0:T(1,128)}, u32[]{:S(2)}) copy-start(s32[1,128]{1,0:T(1,128)} %param.16) | copy-start | bytes 1540
  71.7 11.5 %copy-start.17 = (bf16[2048]{0:T(1024)(128)(2,1)S(1)}, bf16[2048]{0:T(1024)(128)(2,1)}, u32[]{:S(2)}) copy-start(bf16[2048]{0:T(1024)(128)(2,1)} %param.18) | copy-start | bytes 12292
  71.7 13.1 %copy-start.16 = (bf16[2048]{0:T(1024)(128)(2,1)S(1)}, bf16[2048]{0:T(1024)(128)(2,1)}, u32[]{:S(2)}) copy-start(bf16[2048]{0:T(1024)(128)(2,1)} %param.17) | copy-start | bytes 12292
  71.7 15.2 %copy-start.9 = (bf16[256,2048]{1,0:T(8,128)(2,1)S(1)}, bf16[256,2048]{1,0:T(8,128)(2,1)}, u32[]{:S(2)}) copy-start(bf16[256,2048]{1,0:T(8,128)(2,1)} %param.19) | copy-start | bytes 3145732
  81.6 5.9 %copy-start.12 = (bf16[256,512]{1,0:T(8,128)(2,1)S(1)}, bf16[256,512]{1,0:T(8,128)(2,1)}, u32[]{:S(2)}) copy-start(bf16[256,512]{1,0:T(8,128)(2,1)} %param.20) | copy-start | bytes 786436
  81.6 92.9 %collective-permute-start.18 = (f32[1,128]{1,0:T(1,128)}, f32[1,128]{1,0:T(1,128)}, u32[]{:S(2)}, u32[]{:S(2)}) collective-permute-start(f32[1,128]{1,0:T(1,128)} %get-tuple-element.67), channel_id=1, source_target_pairs={{0,2},{2,0},{4,6},{6,4},{8,10},{10,8},{12,14},{14,12},{16,18},{18,... | collective-permute-start | bytes 1544 | tf_op jit(solution)/shard_map/ppermute | solution.py:346
  81.6 94.3 %collective-permute-start.19 = (f32[1,128]{1,0:T(1,128)}, f32[1,128]{1,0:T(1,128)}, u32[]{:S(2)}, u32[]{:S(2)}) collective-permute-start(f32[1,128]{1,0:T(1,128)} %get-tuple-element.67), channel_id=1, source_target_pairs={{0,4},{2,6},{4,0},{6,2},{8,12},{10,14},{12,8},{14,10},{16,20},{18,... | collective-permute-start | bytes 1544 | tf_op jit(solution)/shard_map/ppermute | solution.py:346
  83.1 13.9 %collective-permute-start.1 = (bf16[2048]{0:T(1024)(128)(2,1)S(1)}, bf16[2048]{0:T(1024)(128)(2,1)S(1)}, u32[]{:S(2)}, u32[]{:S(2)}) collective-permute-start(bf16[2048]{0:T(1024)(128)(2,1)S(1)} %copy-done.17), channel_id=1, source_target_pairs={{0,1},{1,0},{2,3},{3,2},{4,5},{5,4},{6,7},{7,6},{8,9},{9,8},{10,11... | collective-permute-start | bytes 12296 | tf_op jit(solution)/shard_map/ppermute | solution.py:28
  84.8 13.9 %collective-permute-start.13 = (bf16[2048]{0:T(1024)(128)(2,1)S(1)}, bf16[2048]{0:T(1024)(128)(2,1)}, u32[]{:S(2)}, u32[]{:S(2)}) collective-permute-start(bf16[2048]{0:T(1024)(128)(2,1)S(1)} %copy-done.16), channel_id=1, source_target_pairs={{0,1},{1,0},{2,3},{3,2},{4,5},{5,4},{6,7},{7,6},{8,9},{9,8},{10,11... | collective-permute-start | bytes 12296 | tf_op jit(solution)/shard_map/ppermute | solution.py:28
  85.2 49.0 %collective-permute-start.12 = (bf16[512,2048]{1,0:T(8,128)(2,1)}, bf16[512,2048]{1,0:T(8,128)(2,1)}, u32[]{:S(2)}, u32[]{:S(2)}) collective-permute-start(bf16[512,2048]{1,0:T(8,128)(2,1)} %param.13), channel_id=1, source_target_pairs={{0,1},{1,0},{2,3},{3,2},{4,5},{5,4},{6,7},{7,6},{8,9},{9,8},{10,11... | collective-permute-start | bytes 6291464 | tf_op jit(solution)/shard_map/ppermute | solution.py:28
  89.8 6.6 %copy-start.18 = (s32[128]{0:T(128)S(1)}, s32[128]{0:T(128)}, u32[]{:S(2)}) copy-start(s32[128]{0:T(128)} %get-tuple-element.66) | copy-start | bytes 1540
  89.8 52.7 %all-to-all-start = ((bf16[16,256,192]{1,2,0:T(8,128)(2,1)}), bf16[16,256,192]{1,2,0:T(8,128)(2,1)}, u32[]{:S(2)}, u32[]{:S(2)}) async-start(bf16[16,256,192]{1,2,0:T(8,128)(2,1)} %pad_maximum_fusion.1), calls=%async_computation | async-start | bytes 3145728 | tf_op jit(solution)/shard_map/all_to_all | solution.py:283
  97.1 80.6 %collective-permute-start.20 = (f32[1,128]{1,0:T(1,128)}, f32[1,128]{1,0:T(1,128)S(1)}, u32[]{:S(2)}, u32[]{:S(2)}) collective-permute-start(f32[1,128]{1,0:T(1,128)} %get-tuple-element.67), channel_id=1, source_target_pairs={{0,6},{2,4},{4,2},{6,0},{8,14},{10,12},{12,10},{14,8},{16,22},{18,... | collective-permute-start | bytes 1544 | tf_op jit(solution)/shard_map/ppermute | solution.py:346
  98.7 35.3 %collective-permute-start = (bf16[32,8,128]{2,0,1:T(8,128)(2,1)S(1)}, bf16[32,8,128]{2,0,1:T(8,128)(2,1)S(1)}, u32[]{:S(2)}, u32[]{:S(2)}) collective-permute-start(bf16[32,8,128]{2,0,1:T(8,128)(2,1)S(1)} %bitcast.265), channel_id=1, source_target_pairs={{0,1},{1,0},{2,3},{3,2},{4,5},{5,4},{6,7},{7,6},{8,9},{9,8},{10,11... | collective-permute-start | bytes 196616 | tf_op jit(solution)/shard_map/ppermute | solution.py:28
  100.1 39.0 %copy-start.15 = (f32[16,1,128]{2,1,0:T(1,128)}, f32[16,1,128]{2,1,0:T(1,128)S(1)}, u32[]{:S(2)}) copy-start(f32[16,1,128]{2,1,0:T(1,128)S(1)} %fusion.36) | copy-start | bytes 24580
  140.8 4.1 %collective-permute-start.7 = (f32[32,384]{1,0:T(8,128)S(1)}, f32[32,384]{1,0:T(8,128)S(1)}, u32[]{:S(2)}, u32[]{:S(2)}) collective-permute-start(f32[32,384]{1,0:T(8,128)S(1)} %pad_maximum_fusion.13), channel_id=1, source_target_pairs={{0,1},{1,0},{2,3},{3,2},{4,5},{5,4},{6,7},{7,6},{8,9},{9,8},{10,11... | collective-permute-start | bytes 147464 | tf_op jit(solution)/shard_map/ppermute | solution.py:28
  144.9 8.7 %collective-permute-start.8 = (f32[1,32,384]{2,1,0:T(8,128)S(1)}, f32[1,32,384]{2,1,0:T(8,128)S(1)}, u32[]{:S(2)}, u32[]{:S(2)}) collective-permute-start(f32[1,32,384]{2,1,0:T(8,128)S(1)} %add_bitcast_fusion), channel_id=1, source_target_pairs={{0,16},{2,18},{4,20},{6,22},{8,24},{10,26},{12,28},{14,30},{16,0},... | collective-permute-start | bytes 147464 | tf_op jit(solution)/shard_map/ppermute | solution.py:73
  153.6 24.8 %collective-permute-start.9 = (f32[2,32,384]{2,1,0:T(8,128)S(1)}, f32[2,32,384]{2,1,0:T(8,128)S(1)}, u32[]{:S(2)}, u32[]{:S(2)}) collective-permute-start(f32[2,32,384]{2,1,0:T(8,128)S(1)} %maximum_bitcast_fusion.1), channel_id=1, source_target_pairs={{0,8},{2,10},{4,12},{6,14},{8,0},{10,2},{12,4},{14,6},{16,24},{18,... | collective-permute-start | bytes 294920 | tf_op jit(solution)/shard_map/ppermute | solution.py:73
  173.3 31.4 %collective-permute-start.15 = (bf16[1024,192]{0,1:T(8,128)(2,1)S(1)}, bf16[1024,192]{0,1:T(8,128)(2,1)S(1)}, u32[]{:S(2)}, u32[]{:S(2)}) collective-permute-start(bf16[1024,192]{0,1:T(8,128)(2,1)S(1)} %constant_dynamic-update-slice_fusion), channel_id=1, source_target_pairs={{0,8},{2,10},{4,12},{6,14},{8,0},{10,2},{12,4},{14,6},{16,24},{18,... | collective-permute-start | bytes 1179656 | tf_op jit(solution)/shard_map/ppermute | solution.py:328
  174.6 43.7 %collective-permute-start.16 = (bf16[1024,192]{0,1:T(8,128)(2,1)S(1)}, bf16[1024,192]{0,1:T(8,128)(2,1)S(1)}, u32[]{:S(2)}, u32[]{:S(2)}) collective-permute-start(bf16[1024,192]{0,1:T(8,128)(2,1)S(1)} %constant_dynamic-update-slice_fusion), channel_id=1, source_target_pairs={{0,16},{2,18},{4,20},{6,22},{8,24},{10,26},{12,28},{14,30},{16,0},... | collective-permute-start | bytes 1179656 | tf_op jit(solution)/shard_map/ppermute | solution.py:328
  176.0 48.3 %collective-permute-start.17 = (bf16[1024,192]{0,1:T(8,128)(2,1)S(1)}, bf16[1024,192]{0,1:T(8,128)(2,1)S(1)}, u32[]{:S(2)}, u32[]{:S(2)}) collective-permute-start(bf16[1024,192]{0,1:T(8,128)(2,1)S(1)} %constant_dynamic-update-slice_fusion), channel_id=1, source_target_pairs={{0,24},{2,26},{4,28},{6,30},{8,16},{10,18},{12,20},{14,22},{16,8},... | collective-permute-start | bytes 1179656 | tf_op jit(solution)/shard_map/ppermute | solution.py:328
  179.2 73.6 %collective-permute-start.10 = (f32[4,32,384]{2,1,0:T(8,128)}, f32[4,32,384]{2,1,0:T(8,128)}, u32[]{:S(2)}, u32[]{:S(2)}) collective-permute-start(f32[4,32,384]{2,1,0:T(8,128)} %bitcast.30), channel_id=1, source_target_pairs={{0,4},{2,6},{4,0},{6,2},{8,12},{10,14},{12,8},{14,10},{16,20},{18,... | collective-permute-start | bytes 589832 | tf_op jit(solution)/shard_map/ppermute | solution.py:73
  250.4 51.3 %copy-start.6 = (bf16[512,512]{1,0:T(8,128)(2,1)}, bf16[512,512]{1,0:T(8,128)(2,1)S(1)}, u32[]{:S(2)}) copy-start(bf16[512,512]{1,0:T(8,128)(2,1)S(1)} %get-tuple-element.28.refs_0_) | copy-start | bytes 1572868
  250.4 5.1 %collective-permute-start.21 = (bf16[512,512]{1,0:T(8,128)(2,1)}, bf16[512,512]{1,0:T(8,128)(2,1)S(1)}, u32[]{:S(2)}, u32[]{:S(2)}) collective-permute-start(bf16[512,512]{1,0:T(8,128)(2,1)} %get-tuple-element.27), channel_id=1, source_target_pairs={{0,2},{2,0},{4,6},{6,4},{8,10},{10,8},{12,14},{14,12},{16,18},{18,... | collective-permute-start | bytes 1572872 | tf_op jit(solution)/shard_map/ppermute | solution.py:353
  250.4 26.4 %collective-permute-start.22 = (bf16[512,512]{1,0:T(8,128)(2,1)}, bf16[512,512]{1,0:T(8,128)(2,1)}, u32[]{:S(2)}, u32[]{:S(2)}) collective-permute-start(bf16[512,512]{1,0:T(8,128)(2,1)} %get-tuple-element.26), channel_id=1, source_target_pairs={{0,4},{2,6},{4,0},{6,2},{8,12},{10,14},{12,8},{14,10},{16,20},{18,... | collective-permute-start | bytes 1572872 | tf_op jit(solution)/shard_map/ppermute | solution.py:353
  251.2 47.4 %collective-permute-start.23 = (bf16[512,512]{1,0:T(8,128)(2,1)}, bf16[512,512]{1,0:T(8,128)(2,1)}, u32[]{:S(2)}, u32[]{:S(2)}) collective-permute-start(bf16[512,512]{1,0:T(8,128)(2,1)} %get-tuple-element.25), channel_id=1, source_target_pairs={{0,6},{2,4},{4,2},{6,0},{8,14},{10,12},{12,10},{14,8},{16,22},{18,... | collective-permute-start | bytes 1572872 | tf_op jit(solution)/shard_map/ppermute | solution.py:353
  252.2 47.0 %copy-start.3 = (bf16[512,2048]{1,0:T(8,128)(2,1)S(1)}, bf16[512,2048]{1,0:T(8,128)(2,1)}, u32[]{:S(2)}) copy-start(bf16[512,2048]{1,0:T(8,128)(2,1)} %copy-done.1) | copy-start | bytes 6291460
  254.0 47.7 %collective-permute-start.11 = (f32[8,32,384]{2,1,0:T(8,128)S(1)}, f32[8,32,384]{2,1,0:T(8,128)S(1)}, u32[]{:S(2)}, u32[]{:S(2)}) collective-permute-start(f32[8,32,384]{2,1,0:T(8,128)S(1)} %bitcast.244), channel_id=1, source_target_pairs={{0,2},{2,0},{4,6},{6,4},{8,10},{10,8},{12,14},{14,12},{16,18},{18,... | collective-permute-start | bytes 1179656 | tf_op jit(solution)/shard_map/ppermute | solution.py:73
  254.4 55.8 %collective-permute-start.24 = (bf16[512,512]{1,0:T(8,128)(2,1)S(1)}, bf16[512,512]{1,0:T(8,128)(2,1)}, u32[]{:S(2)}, u32[]{:S(2)}) collective-permute-start(bf16[512,512]{1,0:T(8,128)(2,1)S(1)} %get-tuple-element.28.refs_0_), channel_id=1, source_target_pairs={{0,1},{1,0},{2,3},{3,2},{4,5},{5,4},{6,7},{7,6},{8,9},{9,8},{10,11... | collective-permute-start | bytes 1572872 | tf_op jit(solution)/shard_map/ppermute | solution.py:28
  255.5 46.2 %copy-start.11 = (bf16[512,512]{1,0:T(8,128)(2,1)}, bf16[512,512]{1,0:T(8,128)(2,1)S(1)}, u32[]{:S(2)}) copy-start(bf16[512,512]{1,0:T(8,128)(2,1)S(1)} %collective-permute-done.21.refs_1_) | copy-start | bytes 1572868
  255.5 54.7 %collective-permute-start.25 = (bf16[512,512]{1,0:T(8,128)(2,1)S(1)}, bf16[512,512]{1,0:T(8,128)(2,1)}, u32[]{:S(2)}, u32[]{:S(2)}) collective-permute-start(bf16[512,512]{1,0:T(8,128)(2,1)S(1)} %collective-permute-done.21.refs_1_), channel_id=1, source_target_pairs={{0,1},{1,0},{2,3},{3,2},{4,5},{5,4},{6,7},{7,6},{8,9},{9,8},{10,11... | collective-permute-start | bytes 1572872 | tf_op jit(solution)/shard_map/ppermute | solution.py:28
  276.7 33.5 %collective-permute-start.26 = (bf16[512,512]{1,0:T(8,128)(2,1)}, bf16[512,512]{1,0:T(8,128)(2,1)}, u32[]{:S(2)}, u32[]{:S(2)}) collective-permute-start(bf16[512,512]{1,0:T(8,128)(2,1)} %collective-permute-done.22.refs_2_), channel_id=1, source_target_pairs={{0,1},{1,0},{2,3},{3,2},{4,5},{5,4},{6,7},{7,6},{8,9},{9,8},{10,11... | collective-permute-start | bytes 1572872 | tf_op jit(solution)/shard_map/ppermute | solution.py:28
  298.5 14.8 %collective-permute-start.27 = (bf16[512,512]{1,0:T(8,128)(2,1)}, bf16[512,512]{1,0:T(8,128)(2,1)}, u32[]{:S(2)}, u32[]{:S(2)}) collective-permute-start(bf16[512,512]{1,0:T(8,128)(2,1)} %collective-permute-done.23.refs_3_), channel_id=1, source_target_pairs={{0,1},{1,0},{2,3},{3,2},{4,5},{5,4},{6,7},{7,6},{8,9},{9,8},{10,11... | collective-permute-start | bytes 1572872 | tf_op jit(solution)/shard_map/ppermute | solution.py:28
  348.1 26.7 %copy-start.14 = (f32[256,256]{1,0:T(8,128)S(1)}, f32[256,256]{1,0:T(8,128)}, u32[]{:S(2)}) copy-start(f32[256,256]{1,0:T(8,128)} %param.25) | copy-start | bytes 786436
  366.8 3.6 collective-permute-start.30
  369.4 5.4 %collective-permute-start.29 = (bf16[256,256]{1,0:T(8,128)(2,1)S(1)}, bf16[256,256]{1,0:T(8,128)(2,1)S(1)}, u32[]{:S(2)}, u32[]{:S(2)}) collective-permute-start(bf16[256,256]{1,0:T(8,128)(2,1)S(1)} %fusion.26), channel_id=1, source_target_pairs={{0,1},{1,0},{2,3},{3,2},{4,5},{5,4},{6,7},{7,6},{8,9},{9,8},{10,11... | collective-permute-start | bytes 393224 | tf_op jit(solution)/shard_map/ppermute | solution.py:28
  (8 other events, 20.9 us)
Sparse Core Ops, SparseCore 0:
  63.0 46.9 all-gather.3
  112.2 54.0 all-gather.5
  168.5 179.5 all-gather.7

commit v2 on v1

--- a/solution.py
+++ b/solution.py
@@ -172,18 +172,18 @@
 
 def finish_body(place_ref, *refs):
     heads = [refs[:4], refs[4:8]]
-    w_ref, base_ref, gain_ref, score_ref = refs[8:12]
-    o_ref, sum_ref = refs[12:]
+    w_refs = [refs[8:12], refs[12:16]]
+    base_ref, gain_ref, score_ref = refs[16:19]
+    o_ref, sum_ref = refs[19:]
     step = pl.program_id(0)
-    rows = heads[0][0].shape[1]
     residual = base_ref[...].astype(jnp.float32)
     for half in range(2):
         term = None
         for slot in range(4):
-            at = pl.multiple_of((half * 4 + (place_ref[1] ^ slot)) * rows, rows)
+            w_ref = w_refs[half][slot]
             part = jnp.dot(
                 heads[half][slot][...],
-                jnp.concatenate([w_ref[0, pl.ds(at, rows), :], w_ref[1, pl.ds(at, rows), :]], axis=1),
+                jnp.concatenate([w_ref[0], w_ref[1]], axis=1),
                 preferred_element_type=jnp.float32,
             )
             term = part if term is None else term + part
@@ -218,14 +218,20 @@
     scored, sub = score.shape[1:]
 
     whole = pl.BlockSpec((tokens, block), lambda i, s: (0, 0))
+
+    def rows_of(half, slot):
+        return pl.BlockSpec(
+            (2, block, sub), lambda i, s: (i, half * 4 + (s[1] ^ slot), 0)
+        )
+
     return pl.pallas_call(
         finish_body,
         grid_spec=pltpu.PrefetchScalarGridSpec(
             num_scalar_prefetch=1,
             grid=(columns // (2 * sub),),
             in_specs=[whole] * 8
+            + [rows_of(half, slot) for half in range(2) for slot in range(4)]
             + [
-                pl.BlockSpec((2, weights.shape[1], sub), lambda i, s: (i, 0, 0)),
                 pl.BlockSpec((tokens, 2 * sub), lambda i, s: (0, i)),
                 pl.BlockSpec((1, 2 * sub), lambda i, s: (0, i)),
                 pl.BlockSpec((2, scored, sub), lambda i, s: (i, 0, 0)),
@@ -240,7 +246,7 @@
             jax.ShapeDtypeStruct((tokens, sub), jnp.float32),
         ],
         name="finish",
-    )(place, *heads, weights, base, gain, score)
+    )(place, *heads, *[weights] * 8, base, gain, score)
 
 
 def on_device(

time: 385 us -> 385 us (level)
  no operation moved by 1% of the time
where the time goes in v2:
time: 385 us; the launch traced here: 384 us
  waiting for transfers between devices  219 us (57%)
  starting transfers between devices  43.4 us (11%)
  Pallas kernels  39.1 us (10%)
  local copies, waits for them, and re-layouts  36.5 us (9%)
  other arithmetic  24.8 us (6%)
  between operations  14.5 us (4%)
  matrix products  6.35 us (2%)
    ppermute x14, waiting for transfers between devices, swap_tp(): return lax.ppermute(x, 'tp', [(0, 1), (1, 0)])  56.3 us
    ppermute x3, waiting for transfers between devices, on_device(): lax.ppermute(piece, 'patch', xor_pairs(n_p, k * kv_here))  44.3 us
    ppermute x3, waiting for transfers between devices, on_device(): lax.ppermute(attended[j], 'patch', xor_pairs(n_p, j))  41.3 us
    all_gather x1, waiting for transfers between devices, on_device(): out_cols = lax.all_gather(out_rows, 'patch', axis=0, tiled=True)  34.8 us
    ppermute x4, waiting for transfers between devices, reduce_patch(): x = keep + lax.ppermute(send, 'patch', xor_pairs(n, flip))  25.3 us
    pallas_call x1, Pallas kernels, finish(): pl.pallas_call(finish_body, grid_spec=pltpu.PrefetchScalarGridSpec(num_sc...  18.5 us
    ppermute x14, starting transfers between devices, swap_tp(): return lax.ppermute(x, 'tp', [(0, 1), (1, 0)])  16.3 us
    gather x1, local copies, waits for them, and re-layouts, on_device(): jnp.take(unembed, jnp.clip(local, 0, rows_dev - 1), axis=0)  13.4 us
  transfers between devices with their start and end apart: 35, of which 20 were waited for; matrix products, arithmetic and copies ran while one was open for 11% of the time, Pallas kernels for 5%

profile of v2, /device:TPU:0, one launch (start us, length us, event | category | flops | bytes accessed | tf_op | source)
XLA Modules:
  0.0 383.9 jit_solution(9762224559791662385)
XLA Ops:
  7.2 13.4 %gather_fusion = bf16[256,4096]{1,0:T(8,128)(2,1)S(1)} fusion(bf16[4008,4096]{1,0:T(8,128)(2,1)} %param.23, s32[1024]{0:T(1024)S(1)} %pad_clamp_fusion), kind=kCustom, calls=%fused_computation | custom fusion | bytes 4195328 | tf_op jit(solution)/shard_map/jit(_take)/gather | solution.py:366
  23.0 2.3 collective-permute-done.2
  26.7 2.6 collective-permute-start.3
  29.3 12.2 %collective-permute-done.3 = bf16[4,256,256]{2,1,0:T(8,128)(2,1)S(1)} collective-permute-done((bf16[4,256,256]{2,1,0:T(8,128)(2,1)S(1)}, bf16[4,256,256]{2,1,0:T(8,128)(2,1)S(1)}, u32[]{:S(2)}, u32[]{:S(2)}) %collective-permute-start.3) | collective-permute-done | bytes 524320 | tf_op jit(solution)/shard_map/ppermute | solution.py:62
  41.6 2.2 collective-permute-start.4
  43.8 5.7 %collective-permute-done.4 = bf16[2,256,256]{2,1,0:T(8,128)(2,1)S(1)} collective-permute-done((bf16[2,256,256]{2,1,0:T(8,128)(2,1)S(1)}, bf16[2,256,256]{2,1,0:T(8,128)(2,1)S(1)}, u32[]{:S(2)}, u32[]{:S(2)}) %collective-permute-start.4) | collective-permute-done | bytes 262176 | tf_op jit(solution)/shard_map/ppermute | solution.py:62
  49.6 2.8 collective-permute-start.5
  52.5 5.0 %collective-permute-done.5 = bf16[1,256,256]{2,1,0:T(8,128)(2,1)S(1)} collective-permute-done((bf16[1,256,256]{2,1,0:T(8,128)(2,1)S(1)}, bf16[1,256,256]{2,1,0:T(8,128)(2,1)S(1)}, u32[]{:S(2)}, u32[]{:S(2)}) %collective-permute-start.5) | collective-permute-done | bytes 131104 | tf_op jit(solution)/shard_map/ppermute | solution.py:62
  57.8 1.5 collective-permute-start.6
  59.3 2.9 collective-permute-done.6
  63.0 1.6 collective-permute-start.14
  64.5 3.6 collective-permute-done.14
  70.0 1.7 collective-permute-start.28
  72.0 7.3 %collective-permute-done.28 = bf16[2048,128]{1,0:T(8,128)(2,1)S(1)} collective-permute-done((bf16[2048,128]{1,0:T(8,128)(2,1)S(1)}, bf16[2048,128]{1,0:T(8,128)(2,1)S(1)}, u32[]{:S(2)}, u32[]{:S(2)}) %collective-permute-start.28) | collective-permute-done | bytes 524320 | tf_op jit(solution)/shard_map/ppermute | solution.py:28
  81.6 1.5 collective-permute-start.19
  83.1 1.7 collective-permute-start.1
  85.2 1.7 collective-permute-start.12
  89.8 5.9 %all-to-all-start = ((bf16[16,256,192]{1,2,0:T(8,128)(2,1)}), bf16[16,256,192]{1,2,0:T(8,128)(2,1)}, u32[]{:S(2)}, u32[]{:S(2)}) async-start(bf16[16,256,192]{1,2,0:T(8,128)(2,1)} %pad_maximum_fusion.1), calls=%async_computation | async-start | bytes 3145728 | tf_op jit(solution)/shard_map/all_to_all | solution.py:289
  97.1 1.6 collective-permute-start.20
  100.1 33.9 %collective-permute-done = bf16[32,8,128]{2,0,1:T(8,128)(2,1)S(1)} collective-permute-done((bf16[32,8,128]{2,0,1:T(8,128)(2,1)S(1)}, bf16[32,8,128]{2,0,1:T(8,128)(2,1)S(1)}, u32[]{:S(2)}, u32[]{:S(2)}) %collective-permute-start) | collective-permute-done | bytes 65568 | tf_op jit(solution)/shard_map/ppermute | solution.py:28
  134.2 2.5 broadcast_select_fusion.1
  139.1 1.6 convolution_bitcast_fusion
  140.8 1.6 collective-permute-start.7
  142.5 1.7 copy.104
  144.9 1.8 collective-permute-start.8
  146.7 1.7 fusion.8
  148.5 5.1 %collective-permute-done.8 = f32[1,32,384]{2,1,0:T(8,128)S(1)} collective-permute-done((f32[1,32,384]{2,1,0:T(8,128)S(1)}, f32[1,32,384]{2,1,0:T(8,128)S(1)}, u32[]{:S(2)}, u32[]{:S(2)}) %collective-permute-start.8) | collective-permute-done | bytes 49184 | tf_op jit(solution)/shard_map/ppermute | solution.py:73
  154.1 12.2 %all-gather.6.cloned.1.call-done.clean_a.clean_b = bf16[512,4096]{1,0:T(8,128)(2,1)} async-done(((bf16[32,4096]{1,0:T(8,128)(2,1)}), bf16[512,4096]{1,0:T(8,128)(2,1)}) %all-gather.6.cloned.1.call-update) | async-done | bytes 4194320 | tf_op jit(solution)/shard_map/all_gather | solution.py:298
  166.3 3.2 fusion.3
  169.7 3.0 fusion.6
  174.6 1.4 collective-permute-start.16
  176.0 1.8 collective-permute-start.17
  180.0 24.7 %collective-permute-done.15 = bf16[1024,192]{0,1:T(8,128)(2,1)S(1)} collective-permute-done((bf16[1024,192]{0,1:T(8,128)(2,1)S(1)}, bf16[1024,192]{0,1:T(8,128)(2,1)S(1)}, u32[]{:S(2)}, u32[]{:S(2)}) %collective-permute-start.15) | collective-permute-done | bytes 393248 | tf_op jit(solution)/shard_map/ppermute | solution.py:334
  204.7 13.6 %collective-permute-done.16 = bf16[1024,192]{0,1:T(8,128)(2,1)S(1)} collective-permute-done((bf16[1024,192]{0,1:T(8,128)(2,1)S(1)}, bf16[1024,192]{0,1:T(8,128)(2,1)S(1)}, u32[]{:S(2)}, u32[]{:S(2)}) %collective-permute-start.16) | collective-permute-done | bytes 393248 | tf_op jit(solution)/shard_map/ppermute | solution.py:334
  218.2 6.0 %collective-permute-done.17 = bf16[1024,192]{0,1:T(8,128)(2,1)S(1)} collective-permute-done((bf16[1024,192]{0,1:T(8,128)(2,1)S(1)}, bf16[1024,192]{0,1:T(8,128)(2,1)S(1)}, u32[]{:S(2)}, u32[]{:S(2)}) %collective-permute-start.17) | collective-permute-done | bytes 393248 | tf_op jit(solution)/shard_map/ppermute | solution.py:334
  227.0 1.8 copy.90.k_ref
  234.3 13.3 %attend.1 = bf16[4,512,512]{2,1,0:T(8,128)(2,1)} custom-call(bf16[4,2,4,128,128]{4,3,2,1,0:T(8,128)(2,1)} %bitcast.239, bf16[2,4,128,128]{3,2,1,0:T(8,128)(2,1)} %copy.90.k_ref, bf16[2,4,128,128]{3,2,1,0:T(8,128)(2,1)} %copy.91.v_ref, f32[4,128,128]{2,1,0:T(8,128)} %broadcast_in_dim.83.m_ref), custom_call_target="tpu_custom_call" | custom-call | tf_op jit(solution)/shard_map/attend/pallas_call | solution.py:125
  247.6 2.7 slice_bitcast_fusion
  256.4 20.3 %collective-permute-done.22.refs_2_ = bf16[512,512]{1,0:T(8,128)(2,1)} collective-permute-done((bf16[512,512]{1,0:T(8,128)(2,1)}, bf16[512,512]{1,0:T(8,128)(2,1)}, u32[]{:S(2)}, u32[]{:S(2)}) %collective-permute-start.22) | collective-permute-done | bytes 524320 | tf_op jit(solution)/shard_map/ppermute | solution.py:359
  277.6 21.0 %collective-permute-done.23.refs_3_ = bf16[512,512]{1,0:T(8,128)(2,1)} collective-permute-done((bf16[512,512]{1,0:T(8,128)(2,1)}, bf16[512,512]{1,0:T(8,128)(2,1)}, u32[]{:S(2)}, u32[]{:S(2)}) %collective-permute-start.23) | collective-permute-done | bytes 524320 | tf_op jit(solution)/shard_map/ppermute | solution.py:359
  299.3 2.4 pad_maximum_fusion.corrupt_a.corrupt_b
  302.9 7.3 %splice.1.refs_16_ = bf16[512,2048]{1,0:T(8,128)(2,1)} custom-call(s32[2]{0:T(128)} %pad_add_fusion.place_ref, bf16[512,4096]{1,0:T(8,128)(2,1)} %pad_maximum_fusion.corrupt_a.corrupt_b, bf16[512,4096]{1,0:T(8,128)(2,1)} %pad_maximum_fusion.corrupt_a.corrupt_b, bf16[512,4096]{1,0:T(8,128)(2,1)} %all-gather.6.cloned.1.call-done.clean_a.clean_b, ...), custom_call_target="tpu_custom_call" | custom-call | tf_op jit(solution)/shard_map/splice/pallas_call | solution.py:154
  310.2 3.1 collective-permute-done.27.refs_7_
  313.3 34.8 %all-gather.8.cloned.1.call-done = bf16[65536,128]{1,0:T(8,128)(2,1)} async-done(((bf16[4096,128]{1,0:T(8,128)(2,1)}), bf16[65536,128]{1,0:T(8,128)(2,1)}) %all-gather.8.cloned.1.call-update) | async-done | bytes 16777232 | tf_op jit(solution)/shard_map/all_gather | solution.py:311
  348.1 18.5 %finish.1 = (f32[512,256]{1,0:T(8,128)}, f32[512,128]{1,0:T(8,128)}) custom-call(s32[2]{0:T(128)} %pad_add_fusion.place_ref, bf16[512,512]{1,0:T(8,128)(2,1)} %copy-done.6, bf16[512,512]{1,0:T(8,128)(2,1)} %copy-done.11, bf16[512,512]{1,0:T(8,128)(2,1)} %collective-permute-done.22.refs_2_, bf16[512,512]{1,0:T(8,128)(2,1)} %collective-permute-done.23.refs_3_, ...), custom_call_target="tpu_custom_call" | custom-call | tf_op jit(solution)/shard_map/finish/pallas_call | solution.py:227
  367.6 1.5 collective-permute-start.30
  371.3 4.3 %collective-permute-done.29 = bf16[256,256]{1,0:T(8,128)(2,1)S(1)} collective-permute-done((bf16[256,256]{1,0:T(8,128)(2,1)S(1)}, bf16[256,256]{1,0:T(8,128)(2,1)S(1)}, u32[]{:S(2)}, u32[]{:S(2)}) %collective-permute-start.29) | collective-permute-done | bytes 131104 | tf_op jit(solution)/shard_map/ppermute | solution.py:28
  375.6 1.8 fusion.25
  (180 shorter events, 43.6 us)
Async XLA Ops:
  6.5 132.6 %all-gather.4.cloned.1.call-start = ((), (), s32[]{:S(2)}) async-start(), calls=%async_computation.1 | async-start | bytes 1114112 | tf_op jit(solution)/shard_map/all_gather | solution.py:377
  22.5 2.9 collective-permute-start.2
  26.7 14.8 %collective-permute-start.3 = (bf16[4,256,256]{2,1,0:T(8,128)(2,1)S(1)}, bf16[4,256,256]{2,1,0:T(8,128)(2,1)S(1)}, u32[]{:S(2)}, u32[]{:S(2)}) collective-permute-start(bf16[4,256,256]{2,1,0:T(8,128)(2,1)S(1)} %dynamic-slice_bitcast_fusion.1), channel_id=1, source_target_pairs={{0,4},{2,6},{4,0},{6,2},{8,12},{10,14},{12,8},{14,10},{16,20},{18,... | collective-permute-start | bytes 1572872 | tf_op jit(solution)/shard_map/ppermute | solution.py:62
  29.3 33.6 %copy-start.10 = (bf16[2,32,2048]{2,1,0:T(8,128)(2,1)S(1)}, bf16[2,32,2048]{2,1,0:T(8,128)(2,1)}, u32[]{:S(2)}) copy-start(bf16[2,32,2048]{2,1,0:T(8,128)(2,1)} %param.14) | copy-start | bytes 786436
  41.6 7.9 %collective-permute-start.4 = (bf16[2,256,256]{2,1,0:T(8,128)(2,1)S(1)}, bf16[2,256,256]{2,1,0:T(8,128)(2,1)S(1)}, u32[]{:S(2)}, u32[]{:S(2)}) collective-permute-start(bf16[2,256,256]{2,1,0:T(8,128)(2,1)S(1)} %dynamic-slice_bitcast_fusion.2), channel_id=1, source_target_pairs={{0,8},{2,10},{4,12},{6,14},{8,0},{10,2},{12,4},{14,6},{16,24},{18,... | collective-permute-start | bytes 786440 | tf_op jit(solution)/shard_map/ppermute | solution.py:62
  43.8 25.1 %copy-start.8 = (bf16[2048,256]{1,0:T(8,128)(2,1)S(1)}, bf16[2048,256]{1,0:T(8,128)(2,1)}, u32[]{:S(2)}) copy-start(bf16[2048,256]{1,0:T(8,128)(2,1)} %param.22) | copy-start | bytes 3145732
  49.6 7.9 %collective-permute-start.5 = (bf16[1,256,256]{2,1,0:T(8,128)(2,1)S(1)}, bf16[1,256,256]{2,1,0:T(8,128)(2,1)S(1)}, u32[]{:S(2)}, u32[]{:S(2)}) collective-permute-start(bf16[1,256,256]{2,1,0:T(8,128)(2,1)S(1)} %constant_dynamic-slice_fusion.10), channel_id=1, source_target_pairs={{0,16},{2,18},{4,20},{6,22},{8,24},{10,26},{12,28},{14,30},{16,0},... | collective-permute-start | bytes 393224 | tf_op jit(solution)/shard_map/ppermute | solution.py:62
  57.8 4.4 %collective-permute-start.6 = (bf16[256,128]{1,0:T(8,128)(2,1)S(1)}, bf16[256,128]{1,0:T(8,128)(2,1)S(1)}, u32[]{:S(2)}, u32[]{:S(2)}) collective-permute-start(bf16[256,128]{1,0:T(8,128)(2,1)S(1)} %bitcast.273), channel_id=1, source_target_pairs={{0,1},{1,0},{2,3},{3,2},{4,5},{5,4},{6,7},{7,6},{8,9},{9,8},{10,11... | collective-permute-start | bytes 196616 | tf_op jit(solution)/shard_map/ppermute | solution.py:28
  62.9 103.4 %all-gather.6.cloned.1.call-start = ((), (), s32[]{:S(2)}) async-start(), calls=%async_computation.2 | async-start | bytes 4456448 | tf_op jit(solution)/shard_map/all_gather | solution.py:298
  63.0 5.2 %collective-permute-start.14 = (bf16[32,2048]{1,0:T(8,128)(2,1)S(1)}, bf16[32,2048]{1,0:T(8,128)(2,1)S(1)}, u32[]{:S(2)}, u32[]{:S(2)}) collective-permute-start(bf16[32,2048]{1,0:T(8,128)(2,1)S(1)} %get-tuple-element.45), channel_id=1, source_target_pairs={{0,1},{1,0},{2,3},{3,2},{4,5},{5,4},{6,7},{7,6},{8,9},{9,8},{10,11... | collective-permute-start | bytes 393224 | tf_op jit(solution)/shard_map/ppermute | solution.py:28
  68.9 279.2 %all-gather.8.cloned.1.call-start = ((), (), s32[]{:S(2)}) async-start(), calls=%async_computation.3 | async-start | bytes 17825792 | tf_op jit(solution)/shard_map/all_gather | solution.py:311
  70.0 9.2 %collective-permute-start.28 = (bf16[2048,128]{1,0:T(8,128)(2,1)S(1)}, bf16[2048,128]{1,0:T(8,128)(2,1)S(1)}, u32[]{:S(2)}, u32[]{:S(2)}) collective-permute-start(bf16[2048,128]{1,0:T(8,128)(2,1)S(1)} %bitcast.262), channel_id=1, source_target_pairs={{0,1},{1,0},{2,3},{3,2},{4,5},{5,4},{6,7},{7,6},{8,9},{9,8},{10,11... | collective-permute-start | bytes 1572872 | tf_op jit(solution)/shard_map/ppermute | solution.py:28
  71.7 9.4 %copy-start.19 = (s32[1,128]{1,0:T(1,128)S(1)}, s32[1,128]{1,0:T(1,128)}, u32[]{:S(2)}) copy-start(s32[1,128]{1,0:T(1,128)} %param.16) | copy-start | bytes 1540
  71.7 11.5 %copy-start.17 = (bf16[2048]{0:T(1024)(128)(2,1)S(1)}, bf16[2048]{0:T(1024)(128)(2,1)}, u32[]{:S(2)}) copy-start(bf16[2048]{0:T(1024)(128)(2,1)} %param.18) | copy-start | bytes 12292
  71.7 13.1 %copy-start.16 = (bf16[2048]{0:T(1024)(128)(2,1)S(1)}, bf16[2048]{0:T(1024)(128)(2,1)}, u32[]{:S(2)}) copy-start(bf16[2048]{0:T(1024)(128)(2,1)} %param.17) | copy-start | bytes 12292
  71.7 15.2 %copy-start.9 = (bf16[256,2048]{1,0:T(8,128)(2,1)S(1)}, bf16[256,2048]{1,0:T(8,128)(2,1)}, u32[]{:S(2)}) copy-start(bf16[256,2048]{1,0:T(8,128)(2,1)} %param.19) | copy-start | bytes 3145732
  81.6 5.9 %copy-start.12 = (bf16[256,512]{1,0:T(8,128)(2,1)S(1)}, bf16[256,512]{1,0:T(8,128)(2,1)}, u32[]{:S(2)}) copy-start(bf16[256,512]{1,0:T(8,128)(2,1)} %param.20) | copy-start | bytes 786436
  81.6 92.9 %collective-permute-start.18 = (f32[1,128]{1,0:T(1,128)}, f32[1,128]{1,0:T(1,128)}, u32[]{:S(2)}, u32[]{:S(2)}) collective-permute-start(f32[1,128]{1,0:T(1,128)} %get-tuple-element.67), channel_id=1, source_target_pairs={{0,2},{2,0},{4,6},{6,4},{8,10},{10,8},{12,14},{14,12},{16,18},{18,... | collective-permute-start | bytes 1544 | tf_op jit(solution)/shard_map/ppermute | solution.py:352
  81.6 94.3 %collective-permute-start.19 = (f32[1,128]{1,0:T(1,128)}, f32[1,128]{1,0:T(1,128)}, u32[]{:S(2)}, u32[]{:S(2)}) collective-permute-start(f32[1,128]{1,0:T(1,128)} %get-tuple-element.67), channel_id=1, source_target_pairs={{0,4},{2,6},{4,0},{6,2},{8,12},{10,14},{12,8},{14,10},{16,20},{18,... | collective-permute-start | bytes 1544 | tf_op jit(solution)/shard_map/ppermute | solution.py:352
  83.1 13.9 %collective-permute-start.1 = (bf16[2048]{0:T(1024)(128)(2,1)S(1)}, bf16[2048]{0:T(1024)(128)(2,1)S(1)}, u32[]{:S(2)}, u32[]{:S(2)}) collective-permute-start(bf16[2048]{0:T(1024)(128)(2,1)S(1)} %copy-done.17), channel_id=1, source_target_pairs={{0,1},{1,0},{2,3},{3,2},{4,5},{5,4},{6,7},{7,6},{8,9},{9,8},{10,11... | collective-permute-start | bytes 12296 | tf_op jit(solution)/shard_map/ppermute | solution.py:28
  84.8 13.9 %collective-permute-start.13 = (bf16[2048]{0:T(1024)(128)(2,1)S(1)}, bf16[2048]{0:T(1024)(128)(2,1)}, u32[]{:S(2)}, u32[]{:S(2)}) collective-permute-start(bf16[2048]{0:T(1024)(128)(2,1)S(1)} %copy-done.16), channel_id=1, source_target_pairs={{0,1},{1,0},{2,3},{3,2},{4,5},{5,4},{6,7},{7,6},{8,9},{9,8},{10,11... | collective-permute-start | bytes 12296 | tf_op jit(solution)/shard_map/ppermute | solution.py:28
  85.2 49.0 %collective-permute-start.12 = (bf16[512,2048]{1,0:T(8,128)(2,1)}, bf16[512,2048]{1,0:T(8,128)(2,1)}, u32[]{:S(2)}, u32[]{:S(2)}) collective-permute-start(bf16[512,2048]{1,0:T(8,128)(2,1)} %param.13), channel_id=1, source_target_pairs={{0,1},{1,0},{2,3},{3,2},{4,5},{5,4},{6,7},{7,6},{8,9},{9,8},{10,11... | collective-permute-start | bytes 6291464 | tf_op jit(solution)/shard_map/ppermute | solution.py:28
  89.8 6.6 %copy-start.18 = (s32[128]{0:T(128)S(1)}, s32[128]{0:T(128)}, u32[]{:S(2)}) copy-start(s32[128]{0:T(128)} %get-tuple-element.66) | copy-start | bytes 1540
  89.8 52.7 %all-to-all-start = ((bf16[16,256,192]{1,2,0:T(8,128)(2,1)}), bf16[16,256,192]{1,2,0:T(8,128)(2,1)}, u32[]{:S(2)}, u32[]{:S(2)}) async-start(bf16[16,256,192]{1,2,0:T(8,128)(2,1)} %pad_maximum_fusion.1), calls=%async_computation | async-start | bytes 3145728 | tf_op jit(solution)/shard_map/all_to_all | solution.py:289
  97.1 80.6 %collective-permute-start.20 = (f32[1,128]{1,0:T(1,128)}, f32[1,128]{1,0:T(1,128)S(1)}, u32[]{:S(2)}, u32[]{:S(2)}) collective-permute-start(f32[1,128]{1,0:T(1,128)} %get-tuple-element.67), channel_id=1, source_target_pairs={{0,6},{2,4},{4,2},{6,0},{8,14},{10,12},{12,10},{14,8},{16,22},{18,... | collective-permute-start | bytes 1544 | tf_op jit(solution)/shard_map/ppermute | solution.py:352
  98.7 35.3 %collective-permute-start = (bf16[32,8,128]{2,0,1:T(8,128)(2,1)S(1)}, bf16[32,8,128]{2,0,1:T(8,128)(2,1)S(1)}, u32[]{:S(2)}, u32[]{:S(2)}) collective-permute-start(bf16[32,8,128]{2,0,1:T(8,128)(2,1)S(1)} %bitcast.272), channel_id=1, source_target_pairs={{0,1},{1,0},{2,3},{3,2},{4,5},{5,4},{6,7},{7,6},{8,9},{9,8},{10,11... | collective-permute-start | bytes 196616 | tf_op jit(solution)/shard_map/ppermute | solution.py:28
  100.1 39.0 %copy-start.15 = (f32[16,1,128]{2,1,0:T(1,128)}, f32[16,1,128]{2,1,0:T(1,128)S(1)}, u32[]{:S(2)}) copy-start(f32[16,1,128]{2,1,0:T(1,128)S(1)} %fusion.36) | copy-start | bytes 24580
  140.8 4.1 %collective-permute-start.7 = (f32[32,384]{1,0:T(8,128)S(1)}, f32[32,384]{1,0:T(8,128)S(1)}, u32[]{:S(2)}, u32[]{:S(2)}) collective-permute-start(f32[32,384]{1,0:T(8,128)S(1)} %pad_maximum_fusion.13), channel_id=1, source_target_pairs={{0,1},{1,0},{2,3},{3,2},{4,5},{5,4},{6,7},{7,6},{8,9},{9,8},{10,11... | collective-permute-start | bytes 147464 | tf_op jit(solution)/shard_map/ppermute | solution.py:28
  144.9 8.7 %collective-permute-start.8 = (f32[1,32,384]{2,1,0:T(8,128)S(1)}, f32[1,32,384]{2,1,0:T(8,128)S(1)}, u32[]{:S(2)}, u32[]{:S(2)}) collective-permute-start(f32[1,32,384]{2,1,0:T(8,128)S(1)} %add_bitcast_fusion), channel_id=1, source_target_pairs={{0,16},{2,18},{4,20},{6,22},{8,24},{10,26},{12,28},{14,30},{16,0},... | collective-permute-start | bytes 147464 | tf_op jit(solution)/shard_map/ppermute | solution.py:73
  153.6 24.8 %collective-permute-start.9 = (f32[2,32,384]{2,1,0:T(8,128)S(1)}, f32[2,32,384]{2,1,0:T(8,128)S(1)}, u32[]{:S(2)}, u32[]{:S(2)}) collective-permute-start(f32[2,32,384]{2,1,0:T(8,128)S(1)} %maximum_bitcast_fusion.1), channel_id=1, source_target_pairs={{0,8},{2,10},{4,12},{6,14},{8,0},{10,2},{12,4},{14,6},{16,24},{18,... | collective-permute-start | bytes 294920 | tf_op jit(solution)/shard_map/ppermute | solution.py:73
  173.3 31.4 %collective-permute-start.15 = (bf16[1024,192]{0,1:T(8,128)(2,1)S(1)}, bf16[1024,192]{0,1:T(8,128)(2,1)S(1)}, u32[]{:S(2)}, u32[]{:S(2)}) collective-permute-start(bf16[1024,192]{0,1:T(8,128)(2,1)S(1)} %constant_dynamic-update-slice_fusion), channel_id=1, source_target_pairs={{0,8},{2,10},{4,12},{6,14},{8,0},{10,2},{12,4},{14,6},{16,24},{18,... | collective-permute-start | bytes 1179656 | tf_op jit(solution)/shard_map/ppermute | solution.py:334
  174.6 43.7 %collective-permute-start.16 = (bf16[1024,192]{0,1:T(8,128)(2,1)S(1)}, bf16[1024,192]{0,1:T(8,128)(2,1)S(1)}, u32[]{:S(2)}, u32[]{:S(2)}) collective-permute-start(bf16[1024,192]{0,1:T(8,128)(2,1)S(1)} %constant_dynamic-update-slice_fusion), channel_id=1, source_target_pairs={{0,16},{2,18},{4,20},{6,22},{8,24},{10,26},{12,28},{14,30},{16,0},... | collective-permute-start | bytes 1179656 | tf_op jit(solution)/shard_map/ppermute | solution.py:334
  176.0 48.3 %collective-permute-start.17 = (bf16[1024,192]{0,1:T(8,128)(2,1)S(1)}, bf16[1024,192]{0,1:T(8,128)(2,1)S(1)}, u32[]{:S(2)}, u32[]{:S(2)}) collective-permute-start(bf16[1024,192]{0,1:T(8,128)(2,1)S(1)} %constant_dynamic-update-slice_fusion), channel_id=1, source_target_pairs={{0,24},{2,26},{4,28},{6,30},{8,16},{10,18},{12,20},{14,22},{16,8},... | collective-permute-start | bytes 1179656 | tf_op jit(solution)/shard_map/ppermute | solution.py:334
  179.2 73.6 %collective-permute-start.10 = (f32[4,32,384]{2,1,0:T(8,128)}, f32[4,32,384]{2,1,0:T(8,128)}, u32[]{:S(2)}, u32[]{:S(2)}) collective-permute-start(f32[4,32,384]{2,1,0:T(8,128)} %bitcast.30), channel_id=1, source_target_pairs={{0,4},{2,6},{4,0},{6,2},{8,12},{10,14},{12,8},{14,10},{16,20},{18,... | collective-permute-start | bytes 589832 | tf_op jit(solution)/shard_map/ppermute | solution.py:73
  250.4 51.3 %copy-start.6 = (bf16[512,512]{1,0:T(8,128)(2,1)}, bf16[512,512]{1,0:T(8,128)(2,1)S(1)}, u32[]{:S(2)}) copy-start(bf16[512,512]{1,0:T(8,128)(2,1)S(1)} %get-tuple-element.28.refs_0_) | copy-start | bytes 1572868
  250.4 5.1 %collective-permute-start.21 = (bf16[512,512]{1,0:T(8,128)(2,1)}, bf16[512,512]{1,0:T(8,128)(2,1)S(1)}, u32[]{:S(2)}, u32[]{:S(2)}) collective-permute-start(bf16[512,512]{1,0:T(8,128)(2,1)} %get-tuple-element.27), channel_id=1, source_target_pairs={{0,2},{2,0},{4,6},{6,4},{8,10},{10,8},{12,14},{14,12},{16,18},{18,... | collective-permute-start | bytes 1572872 | tf_op jit(solution)/shard_map/ppermute | solution.py:359
  250.4 26.4 %collective-permute-start.22 = (bf16[512,512]{1,0:T(8,128)(2,1)}, bf16[512,512]{1,0:T(8,128)(2,1)}, u32[]{:S(2)}, u32[]{:S(2)}) collective-permute-start(bf16[512,512]{1,0:T(8,128)(2,1)} %get-tuple-element.26), channel_id=1, source_target_pairs={{0,4},{2,6},{4,0},{6,2},{8,12},{10,14},{12,8},{14,10},{16,20},{18,... | collective-permute-start | bytes 1572872 | tf_op jit(solution)/shard_map/ppermute | solution.py:359
  251.2 47.4 %collective-permute-start.23 = (bf16[512,512]{1,0:T(8,128)(2,1)}, bf16[512,512]{1,0:T(8,128)(2,1)}, u32[]{:S(2)}, u32[]{:S(2)}) collective-permute-start(bf16[512,512]{1,0:T(8,128)(2,1)} %get-tuple-element.25), channel_id=1, source_target_pairs={{0,6},{2,4},{4,2},{6,0},{8,14},{10,12},{12,10},{14,8},{16,22},{18,... | collective-permute-start | bytes 1572872 | tf_op jit(solution)/shard_map/ppermute | solution.py:359
  252.2 47.0 %copy-start.3 = (bf16[512,2048]{1,0:T(8,128)(2,1)S(1)}, bf16[512,2048]{1,0:T(8,128)(2,1)}, u32[]{:S(2)}) copy-start(bf16[512,2048]{1,0:T(8,128)(2,1)} %copy-done.1) | copy-start | bytes 6291460
  254.0 47.7 %collective-permute-start.11 = (f32[8,32,384]{2,1,0:T(8,128)S(1)}, f32[8,32,384]{2,1,0:T(8,128)S(1)}, u32[]{:S(2)}, u32[]{:S(2)}) collective-permute-start(f32[8,32,384]{2,1,0:T(8,128)S(1)} %bitcast.251), channel_id=1, source_target_pairs={{0,2},{2,0},{4,6},{6,4},{8,10},{10,8},{12,14},{14,12},{16,18},{18,... | collective-permute-start | bytes 1179656 | tf_op jit(solution)/shard_map/ppermute | solution.py:73
  254.4 55.8 %collective-permute-start.24 = (bf16[512,512]{1,0:T(8,128)(2,1)S(1)}, bf16[512,512]{1,0:T(8,128)(2,1)}, u32[]{:S(2)}, u32[]{:S(2)}) collective-permute-start(bf16[512,512]{1,0:T(8,128)(2,1)S(1)} %get-tuple-element.28.refs_0_), channel_id=1, source_target_pairs={{0,1},{1,0},{2,3},{3,2},{4,5},{5,4},{6,7},{7,6},{8,9},{9,8},{10,11... | collective-permute-start | bytes 1572872 | tf_op jit(solution)/shard_map/ppermute | solution.py:28
  255.5 46.2 %copy-start.11 = (bf16[512,512]{1,0:T(8,128)(2,1)}, bf16[512,512]{1,0:T(8,128)(2,1)S(1)}, u32[]{:S(2)}) copy-start(bf16[512,512]{1,0:T(8,128)(2,1)S(1)} %collective-permute-done.21.refs_1_) | copy-start | bytes 1572868
  255.5 54.7 %collective-permute-start.25 = (bf16[512,512]{1,0:T(8,128)(2,1)S(1)}, bf16[512,512]{1,0:T(8,128)(2,1)}, u32[]{:S(2)}, u32[]{:S(2)}) collective-permute-start(bf16[512,512]{1,0:T(8,128)(2,1)S(1)} %collective-permute-done.21.refs_1_), channel_id=1, source_target_pairs={{0,1},{1,0},{2,3},{3,2},{4,5},{5,4},{6,7},{7,6},{8,9},{9,8},{10,11... | collective-permute-start | bytes 1572872 | tf_op jit(solution)/shard_map/ppermute | solution.py:28
  276.7 33.5 %collective-permute-start.26 = (bf16[512,512]{1,0:T(8,128)(2,1)}, bf16[512,512]{1,0:T(8,128)(2,1)}, u32[]{:S(2)}, u32[]{:S(2)}) collective-permute-start(bf16[512,512]{1,0:T(8,128)(2,1)} %collective-permute-done.22.refs_2_), channel_id=1, source_target_pairs={{0,1},{1,0},{2,3},{3,2},{4,5},{5,4},{6,7},{7,6},{8,9},{9,8},{10,11... | collective-permute-start | bytes 1572872 | tf_op jit(solution)/shard_map/ppermute | solution.py:28
  298.5 14.8 %collective-permute-start.27 = (bf16[512,512]{1,0:T(8,128)(2,1)}, bf16[512,512]{1,0:T(8,128)(2,1)}, u32[]{:S(2)}, u32[]{:S(2)}) collective-permute-start(bf16[512,512]{1,0:T(8,128)(2,1)} %collective-permute-done.23.refs_3_), channel_id=1, source_target_pairs={{0,1},{1,0},{2,3},{3,2},{4,5},{5,4},{6,7},{7,6},{8,9},{9,8},{10,11... | collective-permute-start | bytes 1572872 | tf_op jit(solution)/shard_map/ppermute | solution.py:28
  348.1 27.5 %copy-start.14 = (f32[256,256]{1,0:T(8,128)S(1)}, f32[256,256]{1,0:T(8,128)}, u32[]{:S(2)}) copy-start(f32[256,256]{1,0:T(8,128)} %param.25) | copy-start | bytes 786436
  367.6 3.6 collective-permute-start.30
  370.2 5.4 %collective-permute-start.29 = (bf16[256,256]{1,0:T(8,128)(2,1)S(1)}, bf16[256,256]{1,0:T(8,128)(2,1)S(1)}, u32[]{:S(2)}, u32[]{:S(2)}) collective-permute-start(bf16[256,256]{1,0:T(8,128)(2,1)S(1)} %fusion.26), channel_id=1, source_target_pairs={{0,1},{1,0},{2,3},{3,2},{4,5},{5,4},{6,7},{7,6},{8,9},{9,8},{10,11... | collective-permute-start | bytes 393224 | tf_op jit(solution)/shard_map/ppermute | solution.py:28
  (8 other events, 20.9 us)
Sparse Core Ops, SparseCore 0:
  63.0 46.9 all-gather.3
  112.2 54.0 all-gather.5
  168.5 179.5 all-gather.7
